TPU v7x, 8 devices: a whole 2x2x1 slice. The times are simulated.
8 devices in a mesh: dp: 2 (over z, y), tp: 4 (over x, core).
Axes of the slice: x: 2, y: 2, z: 1, core: 2. Of those that a mesh axis runs over, the one named last changes fastest.
Arguments:
- hidden: bfloat16 [2, 64, 4096], P('dp', 'tp'), parts along dimension 0
- vision: bfloat16 [2, 256, 4096], P('dp', 'tp'), parts along dimension 0
- positions: int32 [2, 64], P('dp', 'tp'), parts along dimension 0
- tile_mask: int32 [2, 64, 4], P('dp', 'tp'), parts along dimension 0
- ln1_a: bfloat16 [4096], replicated
- wq_a: bfloat16 [4096, 4096], P(None, 'tp')
- wk_a: bfloat16 [4096, 1024], P(None, 'tp')
- wv_a: bfloat16 [4096, 1024], P(None, 'tp')
- wo_a: bfloat16 [4096, 4096], P('tp')
- ln2_a: bfloat16 [4096], replicated
- wg_a: bfloat16 [4096, 14336], P(None, 'tp')
- wu_a: bfloat16 [4096, 14336], P(None, 'tp')
- wd_a: bfloat16 [14336, 4096], P('tp')
- ln1_b: bfloat16 [4096], replicated
- wq_b: bfloat16 [4096, 4096], P(None, 'tp')
- q_norm: bfloat16 [128], replicated
- wk_b: bfloat16 [4096, 1024], P(None, 'tp')
- wv_b: bfloat16 [4096, 1024], P(None, 'tp')
- k_norm: bfloat16 [128], replicated
- wo_b: bfloat16 [4096, 4096], P('tp')
- ln2_b: bfloat16 [4096], replicated
- wg_b: bfloat16 [4096, 14336], P(None, 'tp')
- wu_b: bfloat16 [4096, 14336], P(None, 'tp')
- wd_b: bfloat16 [14336, 4096], P('tp')
- xgates: float32 [2], replicated
Outputs:
- output: bfloat16 [2, 64, 4096], P('dp', 'tp'), parts along dimension 0
There are 2 independent parts. A program takes and returns all parts, laid end to end along the dimension named above; an argument that names none is the same for every part.
All inputs are finite; a program needn't handle non-finite values.
Results may differ from a plain program's by a relative error of at most 0.0161159.
Values are sent between devices in bfloat16 or wider.
A program may use at most 1 GiB of HBM per device.

v0:
```python
import math
import jax
import jax.numpy as jnp
from jax import lax
from jax.sharding import PartitionSpec as P

ROPE_THETA = 500000.0
ROPE_FACTOR = 8.0
LOW_FACTOR = 1.0
HIGH_FACTOR = 4.0
ORIG_CONTEXT = 8192.0
NORM_EPS = 1e-5
MASK_VALUE = -1e30


def rope_table(head_dim):
    low_wave = ORIG_CONTEXT / LOW_FACTOR
    high_wave = ORIG_CONTEXT / HIGH_FACTOR
    freq_list = []
    for freq_idx in range(head_dim // 2):
        base_freq = 1.0 / (ROPE_THETA ** (2.0 * freq_idx / head_dim))
        wave_len = 2.0 * math.pi / base_freq
        if wave_len > low_wave:
            freq_list.append(base_freq / ROPE_FACTOR)
        elif wave_len < high_wave:
            freq_list.append(base_freq)
        else:
            smooth = (ORIG_CONTEXT / wave_len - LOW_FACTOR) / (HIGH_FACTOR - LOW_FACTOR)
            freq_list.append((1.0 - smooth) * base_freq / ROPE_FACTOR + smooth * base_freq)
    return jnp.array(freq_list, dtype=jnp.float32)


def rms_scale(values, norm_gain):
    values = values.astype(jnp.float32)
    mean_sq = jnp.mean(values * values, axis=-1, keepdims=True)
    return values * lax.rsqrt(mean_sq + NORM_EPS) * norm_gain.astype(jnp.float32)


def rotate(values, cos_tab, sin_tab):
    half_dim = values.shape[-1] // 2
    first_half = values[..., :half_dim]
    second_half = values[..., half_dim:]
    return jnp.concatenate([first_half * cos_tab - second_half * sin_tab, second_half * cos_tab + first_half * sin_tab], axis=-1)


def self_attend(queries, key_vecs, val_vecs):
    seq_len = queries.shape[3]
    head_dim = queries.shape[4]
    scores = jnp.einsum('bgrtd,bsgd->bgrts', queries, key_vecs, preferred_element_type=jnp.float32) * (head_dim ** -0.5)
    causal = lax.broadcasted_iota(jnp.int32, (seq_len, seq_len), 0) >= lax.broadcasted_iota(jnp.int32, (seq_len, seq_len), 1)
    weights = jax.nn.softmax(jnp.where(causal, scores, MASK_VALUE), axis=-1).astype(jnp.bfloat16)
    return jnp.einsum('bgrts,bsgd->bgrtd', weights, val_vecs, preferred_element_type=jnp.float32).astype(jnp.bfloat16)


def cross_attend(queries, key_vecs, val_vecs, visible):
    batch_len, kv_groups, rep_heads, seq_len, head_dim = queries.shape
    vis_len = key_vecs.shape[1]
    tile_count = visible.shape[2]
    scores = jnp.einsum('bgrtd,bsgd->bgrts', queries, key_vecs, preferred_element_type=jnp.float32) * (head_dim ** -0.5)
    scores = scores.reshape(batch_len, kv_groups, rep_heads, seq_len, tile_count, vis_len // tile_count)
    scores = jnp.where(visible[:, None, None, :, :, None], scores, MASK_VALUE)
    weights = jax.nn.softmax(scores.reshape(batch_len, kv_groups, rep_heads, seq_len, vis_len), axis=-1).astype(jnp.bfloat16)
    return jnp.einsum('bgrts,bsgd->bgrtd', weights, val_vecs, preferred_element_type=jnp.float32).astype(jnp.bfloat16)


def gather_rows(values):
    return lax.all_gather(values, 'tp', axis=1, tiled=True)


def scatter_sum(partial):
    return lax.psum_scatter(partial, 'tp', scatter_dimension=1, tiled=True).astype(jnp.float32)


def gated_mlp(resid, norm_gain, w_gate, w_up, w_down):
    gathered = gather_rows(rms_scale(resid, norm_gain).astype(jnp.bfloat16))
    gate_proj = jnp.einsum('btd,df->btf', gathered, w_gate, preferred_element_type=jnp.float32)
    up_proj = jnp.einsum('btd,df->btf', gathered, w_up, preferred_element_type=jnp.float32)
    activated = (jax.nn.silu(gate_proj) * up_proj).astype(jnp.bfloat16)
    partial = jnp.einsum('btf,fd->btd', activated, w_down, preferred_element_type=jnp.float32).astype(jnp.bfloat16)
    return scatter_sum(partial)


def solution(mesh):
    act_spec = P('dp', 'tp', None)
    col_spec = P(None, 'tp')
    row_spec = P('tp', None)
    layer_a = (P(), col_spec, col_spec, col_spec, row_spec, P(), col_spec, col_spec, row_spec)
    layer_b = (P(), col_spec, P(), col_spec, col_spec, P(), row_spec, P(), col_spec, col_spec, row_spec, P())
    in_specs = (act_spec, act_spec, P('dp', 'tp'), act_spec) + layer_a + layer_b

    def body(hidden, vision, positions, tile_mask, ln1_a, wq_a, wk_a, wv_a, wo_a, ln2_a, wg_a, wu_a, wd_a, ln1_b, wq_b, q_norm, wk_b, wv_b, k_norm, wo_b, ln2_b, wg_b, wu_b, wd_b, xgates):
        head_dim = q_norm.shape[0]
        model_dim = hidden.shape[2]
        kv_local = wk_a.shape[1] // head_dim
        rep_heads = wq_a.shape[1] // head_dim // kv_local
        query_shape = (model_dim, kv_local, rep_heads, head_dim)
        head_shape = (model_dim, kv_local, head_dim)
        out_shape = (kv_local, rep_heads, head_dim, model_dim)
        angles = gather_rows(positions).astype(jnp.float32)[..., None] * rope_table(head_dim)
        cos_tab = jnp.cos(angles)
        sin_tab = jnp.sin(angles)
        gathered = gather_rows(rms_scale(hidden, ln1_a).astype(jnp.bfloat16))
        queries = jnp.einsum('btd,dgre->bgrte', gathered, wq_a.reshape(query_shape), preferred_element_type=jnp.float32)
        queries = rotate(queries, cos_tab[:, None, None], sin_tab[:, None, None]).astype(jnp.bfloat16)
        key_vecs = jnp.einsum('btd,dge->btge', gathered, wk_a.reshape(head_shape), preferred_element_type=jnp.float32)
        key_vecs = rotate(key_vecs, cos_tab[:, :, None], sin_tab[:, :, None]).astype(jnp.bfloat16)
        val_vecs = jnp.einsum('btd,dge->btge', gathered, wv_a.reshape(head_shape), preferred_element_type=jnp.float32).astype(jnp.bfloat16)
        context = self_attend(queries, key_vecs, val_vecs)
        partial = jnp.einsum('bgrtd,grde->bte', context, wo_a.reshape(out_shape), preferred_element_type=jnp.float32).astype(jnp.bfloat16)
        h_one = (hidden.astype(jnp.float32) + scatter_sum(partial)).astype(jnp.bfloat16)
        h_two = (h_one.astype(jnp.float32) + gated_mlp(h_one, ln2_a, wg_a, wu_a, wd_a)).astype(jnp.bfloat16)
        gathered = gather_rows(rms_scale(h_two, ln1_b).astype(jnp.bfloat16))
        queries = jnp.einsum('btd,dgre->bgrte', gathered, wq_b.reshape(query_shape), preferred_element_type=jnp.float32)
        queries = rms_scale(queries, q_norm).astype(jnp.bfloat16)
        vis_full = gather_rows(vision)
        key_vecs = jnp.einsum('bsd,dge->bsge', vis_full, wk_b.reshape(head_shape), preferred_element_type=jnp.float32)
        key_vecs = rms_scale(key_vecs, k_norm).astype(jnp.bfloat16)
        val_vecs = jnp.einsum('bsd,dge->bsge', vis_full, wv_b.reshape(head_shape), preferred_element_type=jnp.float32).astype(jnp.bfloat16)
        context = cross_attend(queries, key_vecs, val_vecs, gather_rows(tile_mask) > 0)
        partial = jnp.einsum('bgrtd,grde->bte', context, wo_b.reshape(out_shape), preferred_element_type=jnp.float32).astype(jnp.bfloat16)
        row_keep = jnp.any(tile_mask > 0, axis=-1, keepdims=True).astype(jnp.float32)
        gate_vals = jnp.tanh(xgates.astype(jnp.float32))
        h_three = (h_two.astype(jnp.float32) + gate_vals[0] * row_keep * scatter_sum(partial)).astype(jnp.bfloat16)
        mlp_out = gated_mlp(h_three, ln2_b, wg_b, wu_b, wd_b)
        return (h_three.astype(jnp.float32) + gate_vals[1] * row_keep * mlp_out).astype(jnp.bfloat16)

    return jax.shard_map(body, mesh=mesh, in_specs=in_specs, out_specs=act_spec, check_vma=False)
```

profile of v0, /device:TPU:0, one launch (start us, length us, event | category | flops | bytes accessed | tf_op | source)
XLA Modules:
  0.0 262.0 jit_solution(3985241309589170614)
XLA Ops:
  6.6 0.8 convert_element_type.151
  7.4 1.0 fusion.81
  8.5 1.0 fusion.83
  9.5 11.9 %all_gather.21 = bf16[1,64,4096]{2,1,0:T(8,128)(2,1)S(1)} all-gather(bf16[1,16,4096]{2,1,0:T(8,128)(2,1)S(1)} %fusion.83), channel_id=1, replica_groups=mesh['dp'=2,'tp'=4] {'tp'}, dimensions={1}, use_global_device_ids=true | all-gather | bytes 655360 | tf_op jit(solution)/shard_map/all_gather | solution.py:67
  21.3 14.3 %reshape.413 = bf16[4096,2,4,128]{3,2,1,0:T(4,128)(2,1)} reshape(bf16[4096,1024]{1,0:T(8,128)(2,1)} %param.31) | data formatting | bytes 16777216 | tf_op jit(solution)/shard_map/reshape | solution.py:103
  35.6 0.6 dynamic-slice
  36.9 0.1 bitcast_dynamic-update-slice_fusion
  37.0 4.5 %all-reduce = s32[64]{0:T(128)S(1)} all-reduce(s32[64]{0:T(128)S(1)} %bitcast_dynamic-update-slice_fusion), channel_id=1, replica_groups=mesh['dp'=2,'tp'=4] {'tp'}, use_global_device_ids=true, to_apply=%add | all-reduce | flops 64 | bytes 512
  41.5 5.1 %fusion.30 = f32[1,2,4,64,128]{4,3,2,1,0:T(8,128)S(1)} fusion(bf16[4096,2,4,128]{3,2,1,0:T(4,128)(2,1)} %reshape.413, bf16[1,64,4096]{2,1,0:T(8,128)(2,1)S(1)} %all_gather.21), kind=kOutput, calls=%fused_computation.37 | convolution fusion | flops 536870912 | bytes 9175040 | tf_op jit(solution)/shard_map/btd,dgre->bgrte/dot_general | solution.py:103
  46.7 0.5 fusion.48
  47.2 0.2 multiply_cosine_fusion
  47.4 0.2 fusion.99
  47.6 0.5 fusion.54
  48.1 0.4 fusion.135
  48.5 5.9 %fusion.13 = bf16[1,64,4096]{2,1,0:T(8,128)(2,1)} fusion(bf16[2,4,128,4096]{3,2,1,0:T(8,128)(2,1)} %bitcast.176, bf16[64,2,128,1]{2,0,3,1:T(8,128)(2,1)S(1)} %fusion.54, f32[2,4,64,64]{2,3,1,0:T(8,128)S(1)} %get-tuple-element.20, f32[2,4,64]{2,1,0:T(4,128)S(1)} %get-tuple-element.19), kind=kOutput, calls=%fused_computation.19 | convolution fusion | flops 545652736 | bytes 9078784 | tf_op jit(solution)/shard_map/bgrtd,grde->bte/dot_general | solution.py:109
  54.5 16.4 %reduce-scatter.5.cloned.1.call-done = bf16[1,16,4096]{2,1,0:T(8,128)(2,1)} async-done(((bf16[1,64,4096]{2,1,0:T(8,128)(2,1)}), bf16[1,16,4096]{2,1,0:T(8,128)(2,1)}) %reduce-scatter.5.cloned.1.call-update) | async-done | bytes 131088 | tf_op jit(solution)/shard_map/reduce_scatter | solution.py:71
  70.9 1.1 fusion.85
  72.0 0.1 fusion.87
  72.1 0.5 copy-done.2
  72.7 9.3 %all_gather.23 = bf16[1,64,4096]{2,1,0:T(8,128)(2,1)S(1)} all-gather(bf16[1,16,4096]{2,1,0:T(8,128)(2,1)S(1)} %fusion.87), channel_id=1, replica_groups=mesh['dp'=2,'tp'=4] {'tp'}, dimensions={1}, use_global_device_ids=true | all-gather | bytes 655360 | tf_op jit(solution)/shard_map/all_gather | solution.py:67
  81.9 12.0 %fusion.75 = f32[64,3584]{1,0:T(8,128)S(1)} fusion(bf16[4096,3584]{1,0:T(8,128)(2,1)} %param.36, bf16[1,64,4096]{2,1,0:T(8,128)(2,1)S(1)} %all_gather.23), kind=kOutput, calls=%fused_computation.65 | convolution fusion | flops 1879048192 | bytes 30801920 | tf_op jit(solution)/shard_map/btd,df->btf/dot_general | solution.py:76
  94.0 22.7 %fusion.10 = bf16[1,64,4096]{2,1,0:T(8,128)(2,1)} fusion(bf16[3584,4096]{1,0:T(8,128)(2,1)} %param.38, bf16[4096,3584]{1,0:T(8,128)(2,1)} %param.37, f32[64,3584]{1,0:T(8,128)S(1)} %fusion.75, bf16[1,64,4096]{2,1,0:T(8,128)(2,1)S(1)} %all_gather.23), kind=kOutput, calls=%fused_computation.16 | convolution fusion | flops 3759734784 | bytes 60686336 | tf_op jit(solution)/shard_map/btf,fd->btd/dot_general | solution.py:79
  116.7 0.7 all-gather.2.cloned.1.call-update
  117.5 14.3 %reshape.419 = bf16[4096,2,4,128]{3,2,1,0:T(4,128)(2,1)} reshape(bf16[4096,1024]{1,0:T(8,128)(2,1)} %param.40) | data formatting | bytes 16777216 | tf_op jit(solution)/shard_map/reshape | solution.py:113
  131.9 7.9 %all_gather.24 = s32[1,64,4]{2,0,1:T(1,128)S(1)} all-gather(s32[1,16,4]{2,0,1:T(1,128)S(1)} %copy.54), channel_id=1, replica_groups=mesh['dp'=2,'tp'=4] {'tp'}, dimensions={1}, use_global_device_ids=true | all-gather | bytes 1280 | tf_op jit(solution)/shard_map/all_gather | solution.py:67
  139.9 0.1 copy.56
  140.0 0.1 broadcast_in_dim.25
  140.2 0.1 broadcast_in_dim.26
  140.4 1.1 fusion.89
  141.4 1.0 fusion.91
  142.4 14.7 %all_gather.25 = bf16[1,64,4096]{2,1,0:T(8,128)(2,1)S(1)} all-gather(bf16[1,16,4096]{2,1,0:T(8,128)(2,1)S(1)} %fusion.91), channel_id=1, replica_groups=mesh['dp'=2,'tp'=4] {'tp'}, dimensions={1}, use_global_device_ids=true | all-gather | bytes 655360 | tf_op jit(solution)/shard_map/all_gather | solution.py:67
  157.2 5.1 %multiply_reduce_fusion.1 = (f32[2,4,64]{2,1,0:T(4,128)S(1)}, f32[2,4,128,1,64]{2,4,1,0,3:T(8,128)S(1)}) fusion(bf16[4096,2,4,128]{3,2,1,0:T(4,128)(2,1)} %reshape.419, bf16[1,64,4096]{2,1,0:T(8,128)(2,1)S(1)} %all_gather.25), kind=kOutput, calls=%fused_computation.104 | convolution fusion | flops 537001472 | bytes 9177088 | tf_op jit(solution)/shard_map/btd,dgre->bgrte/dot_general | solution.py:113
  162.3 2.5 multiply_reduce_fusion
  164.9 0.3 fusion.28
  165.2 0.3 fusion.138
  165.4 2.9 %fusion.43 = bf16[256,2,128,1]{2,0,3,1:T(8,128)(2,1)S(1)} fusion(bf16[1,256,4096]{2,1,0:T(8,128)(2,1)} %all-gather.2.cloned.1.call-done, bf16[4096,256]{1,0:T(8,128)(2,1)} %param.43), kind=kOutput, calls=%fused_computation.45 | convolution fusion | flops 536936448 | bytes 4325376 | tf_op jit(solution)/shard_map/bsd,dge->bsge/dot_general | solution.py:118
  168.4 6.3 %fusion.12 = bf16[1,64,4096]{2,1,0:T(8,128)(2,1)} fusion(bf16[2,4,128,4096]{3,2,1,0:T(8,128)(2,1)} %bitcast.177, bf16[256,2,128,1]{2,0,3,1:T(8,128)(2,1)S(1)} %fusion.43, f32[2,4,64]{2,1,0:T(4,128)S(1)} %fusion.138, f32[2,4,64,256]{3,2,1,0:T(8,128)S(1)} %fusion.28), kind=kOutput, calls=%fused_computation.18 | convolution fusion | flops 571147008 | bytes 9570304 | tf_op jit(solution)/shard_map/bgrtd,grde->bte/dot_general | solution.py:120
  174.8 0.6 fusion.134
  175.4 1.3 broadcast_select_fusion
  176.6 14.3 %reduce-scatter.9.cloned.1.call-done = bf16[1,16,4096]{2,1,0:T(8,128)(2,1)} async-done(((bf16[1,64,4096]{2,1,0:T(8,128)(2,1)}), bf16[1,16,4096]{2,1,0:T(8,128)(2,1)}) %reduce-scatter.9.cloned.1.call-update) | async-done | bytes 131088 | tf_op jit(solution)/shard_map/reduce_scatter | solution.py:71
  191.0 1.1 fusion.93
  192.1 0.1 fusion.95
  192.2 0.5 copy-done.6
  192.7 9.3 %all_gather.27 = bf16[1,64,4096]{2,1,0:T(8,128)(2,1)S(1)} all-gather(bf16[1,16,4096]{2,1,0:T(8,128)(2,1)S(1)} %fusion.95), channel_id=1, replica_groups=mesh['dp'=2,'tp'=4] {'tp'}, dimensions={1}, use_global_device_ids=true | all-gather | bytes 655360 | tf_op jit(solution)/shard_map/all_gather | solution.py:67
  202.0 12.0 %fusion.71 = f32[64,3584]{1,0:T(8,128)S(1)} fusion(bf16[4096,3584]{1,0:T(8,128)(2,1)} %param.47, bf16[1,64,4096]{2,1,0:T(8,128)(2,1)S(1)} %all_gather.27), kind=kOutput, calls=%fused_computation.62 | convolution fusion | flops 1879048192 | bytes 30801920 | tf_op jit(solution)/shard_map/btd,df->btf/dot_general | solution.py:76
  214.1 22.8 %fusion.11 = bf16[1,64,4096]{2,1,0:T(8,128)(2,1)} fusion(bf16[3584,4096]{1,0:T(8,128)(2,1)} %param.49, bf16[4096,3584]{1,0:T(8,128)(2,1)} %param.48, f32[64,3584]{1,0:T(8,128)S(1)} %fusion.71, bf16[1,64,4096]{2,1,0:T(8,128)(2,1)S(1)} %all_gather.27), kind=kOutput, calls=%fused_computation.17 | convolution fusion | flops 3759734784 | bytes 60686336 | tf_op jit(solution)/shard_map/btf,fd->btd/dot_general | solution.py:79
  236.9 16.8 %reduce-scatter.11.cloned.1.call-done = bf16[1,16,4096]{2,1,0:T(8,128)(2,1)} async-done(((bf16[1,64,4096]{2,1,0:T(8,128)(2,1)}), bf16[1,16,4096]{2,1,0:T(8,128)(2,1)}) %reduce-scatter.11.cloned.1.call-update) | async-done | bytes 131088 | tf_op jit(solution)/shard_map/reduce_scatter | solution.py:71
  253.7 1.7 fusion.96
  (67 shorter events, 0.7 us)
Async XLA Ops:
  6.5 155.7 %copy-start = (bf16[4096,256]{1,0:T(8,128)(2,1)S(1)}, bf16[4096,256]{1,0:T(8,128)(2,1)}, u32[]{:S(2)}) copy-start(bf16[4096,256]{1,0:T(8,128)(2,1)} %param.42) | copy-start | bytes 6291460
  6.5 64.4 %reduce-scatter.5.cloned.1.call-start = ((), (), s32[]{:S(2)}) async-start(), calls=%async_computation.4 | async-start | bytes 655360 | tf_op jit(solution)/shard_map/reduce_scatter | solution.py:71
  21.3 14.3 %copy-start.18 = (u32[8]{0:T(128)S(1)}, u32[8]{0:T(128)}, u32[]{:S(2)}) copy-start(u32[8]{0:T(128)} %constant.45) | copy-start | bytes 100
  21.3 15.5 %copy-start.14 = (s32[1,16]{1,0:T(1,128)S(1)}, s32[1,16]{1,0:T(1,128)}, u32[]{:S(2)}) copy-start(s32[1,16]{1,0:T(1,128)} %param.28) | copy-start | bytes 196
  35.6 11.5 %copy-start.11 = (f32[64]{0:T(128)S(1)}, f32[64]{0:T(128)}, u32[]{:S(2)}) copy-start(f32[64]{0:T(128)} %constant.38.clone) | copy-start | bytes 772
  41.5 5.1 %copy-start.12 = (bf16[4096,256]{1,0:T(8,128)(2,1)S(1)}, bf16[4096,256]{1,0:T(8,128)(2,1)}, u32[]{:S(2)}) copy-start(bf16[4096,256]{1,0:T(8,128)(2,1)} %param.32) | copy-start | bytes 6291460
  41.5 6.1 %copy-start.13 = (bf16[4096,256]{1,0:T(8,128)(2,1)S(1)}, bf16[4096,256]{1,0:T(8,128)(2,1)}, u32[]{:S(2)}) copy-start(bf16[4096,256]{1,0:T(8,128)(2,1)} %param.33) | copy-start | bytes 6291460
  46.7 7.8 %copy-start.7 = (bf16[4096]{0:T(1024)(128)(2,1)S(1)}, bf16[4096]{0:T(1024)(128)(2,1)}, u32[]{:S(2)}) copy-start(bf16[4096]{0:T(1024)(128)(2,1)} %param.35) | copy-start | bytes 24580
  46.7 24.3 %copy-start.4 = (bf16[1,16,4096]{2,1,0:T(8,128)(2,1)S(1)}, bf16[1,16,4096]{2,1,0:T(8,128)(2,1)}, u32[]{:S(2)}) copy-start(bf16[1,16,4096]{2,1,0:T(8,128)(2,1)} %param.26) | copy-start | bytes 393220
  54.4 85.9 %reduce-scatter.7.cloned.1.call-start = ((), (), s32[]{:S(2)}) async-start(), calls=%async_computation.5 | async-start | bytes 655360 | tf_op jit(solution)/shard_map/reduce_scatter | solution.py:71
  72.0 0.7 copy-start.2
  93.9 23.5 %copy-start.8 = (bf16[4096]{0:T(1024)(128)(2,1)S(1)}, bf16[4096]{0:T(1024)(128)(2,1)}, u32[]{:S(2)}) copy-start(bf16[4096]{0:T(1024)(128)(2,1)} %param.39) | copy-start | bytes 24580
  116.7 45.6 %all-gather.2.cloned.1.call-start = ((), (), s32[]{:S(2)}) async-start(), calls=%async_computation.6 | async-start | bytes 2621440 | tf_op jit(solution)/shard_map/all_gather | solution.py:67
  117.4 73.5 %reduce-scatter.9.cloned.1.call-start = ((), (), s32[]{:S(2)}) async-start(), calls=%async_computation.7 | async-start | bytes 655360 | tf_op jit(solution)/shard_map/reduce_scatter | solution.py:71
  117.5 14.3 %copy-start.10 = (s32[1,16,4]{1,2,0:T(4,128)S(1)}, s32[1,16,4]{1,2,0:T(4,128)}, u32[]{:S(2)}) copy-start(s32[1,16,4]{1,2,0:T(4,128)} %param.29) | copy-start | bytes 772
  117.5 22.8 %copy-start.15 = (bf16[128]{0:T(256)(128)(2,1)S(1)}, bf16[128]{0:T(256)(128)(2,1)}, u32[]{:S(2)}) copy-start(bf16[128]{0:T(256)(128)(2,1)} %param.41) | copy-start | bytes 772
  117.5 22.8 %copy-start.16 = (bf16[128]{0:T(256)(128)(2,1)S(1)}, bf16[128]{0:T(256)(128)(2,1)}, u32[]{:S(2)}) copy-start(bf16[128]{0:T(256)(128)(2,1)} %param.44) | copy-start | bytes 772
  117.5 22.8 %copy-start.3 = (bf16[1,16,4096]{2,1,0:T(8,128)(2,1)S(1)}, bf16[1,16,4096]{2,1,0:T(8,128)(2,1)}, u32[]{:S(2)}) copy-start(bf16[1,16,4096]{2,1,0:T(8,128)(2,1)} %copy-done.2) | copy-start | bytes 393220
  164.8 9.9 %copy-start.17 = (f32[2]{0:T(128)S(1)}, f32[2]{0:T(128)}, u32[]{:S(2)}) copy-start(f32[2]{0:T(128)} %param.50) | copy-start | bytes 28
  164.8 9.9 %copy-start.9 = (bf16[4096]{0:T(1024)(128)(2,1)S(1)}, bf16[4096]{0:T(1024)(128)(2,1)}, u32[]{:S(2)}) copy-start(bf16[4096]{0:T(1024)(128)(2,1)} %param.46) | copy-start | bytes 24580
  164.9 26.1 %copy-start.5 = (bf16[1,16,4096]{2,1,0:T(8,128)(2,1)S(1)}, bf16[1,16,4096]{2,1,0:T(8,128)(2,1)}, u32[]{:S(2)}) copy-start(bf16[1,16,4096]{2,1,0:T(8,128)(2,1)} %reduce-scatter.7.cloned.1.call-done) | copy-start | bytes 393220
  174.7 79.1 %reduce-scatter.11.cloned.1.call-start = ((), (), s32[]{:S(2)}) async-start(), calls=%async_computation.8 | async-start | bytes 655360 | tf_op jit(solution)/shard_map/reduce_scatter | solution.py:71
  192.1 0.7 copy-start.6
  214.0 41.4 %copy-start.1 = (bf16[4096,256]{1,0:T(8,128)(2,1)S(1)}, bf16[4096,256]{1,0:T(8,128)(2,1)}, u32[]{:S(2)}) copy-start(bf16[4096,256]{1,0:T(8,128)(2,1)} %param.42) | copy-start | bytes 6291460
Sparse Core Ops, SparseCore 0:
  54.5 16.3 reduce-scatter.4
  116.8 16.6 reduce-scatter.6
  135.1 23.7 all-gather.1
  174.8 16.1 reduce-scatter.8
  237.0 16.6 reduce-scatter.10
where the time goes:
time: 263 us; the launch traced here: 262 us
  matrix products  99 us (38%)
  blocking collectives  57.6 us (22%)
  waiting for transfers between devices  48.4 us (18%)
  local copies, waits for them, and re-layouts  31.5 us (12%)
  between operations  14.2 us (5%)
  other arithmetic  11.1 us (4%)
    all_gather x5, blocking collectives, gather_rows(): return lax.all_gather(values, 'tp', axis=1, tiled=True)  53 us
    reduce_scatter x4, waiting for transfers between devices, scatter_sum(): lax.psum_scatter(partial, 'tp', scatter_dimension=1, tiled=True)  47.6 us
    dot_general x2, matrix products, gated_mlp(): jnp.einsum('btf,fd->btd', activated, w_down, preferred_element_type=jnp.f...  45.5 us
    dot_general x2, matrix products, gated_mlp(): jnp.einsum('btd,df->btf', gathered, w_gate, preferred_element_type=jnp.fl...  24 us
    reshape x1, local copies, waits for them, and re-layouts, body(): wq_b.reshape(query_shape)  14.3 us
    reshape x1, local copies, waits for them, and re-layouts, body(): wq_a.reshape(query_shape)  14.3 us
    dot_general x1, matrix products, body(): jnp.einsum('bgrtd,grde->bte', context, wo_b.reshape(out_shape), preferred...  6.28 us
    dot_general x1, matrix products, body(): jnp.einsum('bgrtd,grde->bte', context, wo_a.reshape(out_shape), preferred...  5.93 us
  transfers between devices with their start and end apart: 5, of which 3 were waited for; matrix products, arithmetic and copies ran while one was open for 9% of the time, Pallas kernels for 0%

commit v1 on v0

v1 whole, which is shorter than its diff:
```python
import math
import jax
import jax.numpy as jnp
import numpy as np
from jax import lax
from jax.experimental import pallas as pl
from jax.experimental.pallas import tpu as pltpu
from jax.sharding import PartitionSpec as P

ROPE_THETA = 500000.0
ROPE_FACTOR = 8.0
LOW_FACTOR = 1.0
HIGH_FACTOR = 4.0
ORIG_CONTEXT = 8192.0
NORM_EPS = 1e-5
MASK_VALUE = -1e30
MESH = pl.DeviceIdType.MESH
BF16 = jnp.bfloat16
F32 = jnp.float32

T = 64
TB = 16
D = 4096
V = 256
VB = 64
HD = 128
KV = 2
REP = 4
FF = 3584
NC = 256
SP = 13
WO_ROWS = KV * REP * HD

SEGMENTS = []
_at = 0
for _name, _count in (('qa', 2), ('kva', 1), ('oa', 2), ('gua', 14), ('da', 8),
                      ('kvb', 1), ('qb', 2), ('ob', 2), ('gub', 14), ('db', 8)):
    SEGMENTS.append((_name, _at, _count))
    _at += _count
TOTAL = _at
BASE = {name: first for name, first, _ in SEGMENTS}


def rope_table(head_dim):
    low_wave = ORIG_CONTEXT / LOW_FACTOR
    high_wave = ORIG_CONTEXT / HIGH_FACTOR
    freq_list = []
    for freq_idx in range(head_dim // 2):
        base_freq = 1.0 / (ROPE_THETA ** (2.0 * freq_idx / head_dim))
        wave_len = 2.0 * math.pi / base_freq
        if wave_len > low_wave:
            freq_list.append(base_freq / ROPE_FACTOR)
        elif wave_len < high_wave:
            freq_list.append(base_freq)
        else:
            smooth = (ORIG_CONTEXT / wave_len - LOW_FACTOR) / (HIGH_FACTOR - LOW_FACTOR)
            freq_list.append((1.0 - smooth) * base_freq / ROPE_FACTOR + smooth * base_freq)
    return np.array(freq_list, dtype=np.float32)


def dot(a, b):
    return jnp.dot(a, b, preferred_element_type=F32)


def dot_t(a, b):
    return lax.dot_general(a, b, (((1,), (1,)), ((), ())), preferred_element_type=F32)


def kernel(hid, vis, pos, tmask, freq,
           ln1a, wqa, wka, wva, woa, ln2a, wga, wua, wda,
           ln1b, wqb, qn, wkb, wvb, kn, wob, ln2b, wgb, wub, wdb, xg,
           out,
           wbuf, wsem, hx, posb, maskb, cosb, sinb, h, x, act, ctx, qb, kb, vb, vg,
           pb, rcv1, snd2, rcv2, pf, rcvf,
           lsem, hs, hr, ps, pr, ms, mr, vs, vr, s1, r1, s2, r2, s3, r3, fs, fr):
    d = lax.axis_index('tp')
    core = lax.rem(d, 2)
    part = d + 1 - 2 * core
    cross = lax.rem(d + 2, 4)
    diag = 3 - d
    peers = (part, cross, diag)
    weights = {
        'qa': (wqa,), 'kva': (wka, wva), 'oa': (woa,), 'gua': (wga, wua), 'da': (wda,),
        'qb': (wqb,), 'kvb': (wkb, wvb), 'ob': (wob,), 'gub': (wgb, wub), 'db': (wdb,),
    }

    def cols(index):
        return pl.ds(pl.multiple_of(index * NC, NC), NC)

    def start_segment(name, first, m):
        slot = lax.rem(m, SP)
        i = m - first
        refs = weights[name]
        kind = name[:-1]
        if kind == 'q':
            for half in range(2):
                pltpu.make_async_copy(refs[0].at[:, cols(2 * i + half)], wbuf.at[slot, half], wsem.at[slot, half]).start()
        elif kind == 'kv':
            for half in range(2):
                pltpu.make_async_copy(refs[half], wbuf.at[slot, half], wsem.at[slot, half]).start()
        elif kind == 'gu':
            for half in range(2):
                pltpu.make_async_copy(refs[half].at[:, cols(i)], wbuf.at[slot, half], wsem.at[slot, half]).start()
        elif kind == 'd':
            for half in range(2):
                pltpu.make_async_copy(refs[0].at[:, cols(i + 8 * half)], wbuf.at[slot, half, pl.ds(0, FF)], wsem.at[slot, half]).start()
        else:
            for half in range(2):
                for sub in range(4):
                    pltpu.make_async_copy(refs[0].at[:, cols(4 * i + sub + 8 * half)],
                                          wbuf.at[slot, half, pl.ds(sub * WO_ROWS, WO_ROWS)], wsem.at[slot, half]).start()

    def issue(m, low, high):
        for name, first, count in SEGMENTS:
            if first >= high or first + count <= low:
                continue
            if first <= low and high <= first + count:
                start_segment(name, first, m)
            else:
                @pl.when(jnp.logical_and(m >= first, m < first + count))
                def _():
                    start_segment(name, first, m)

    def refill(m, low, high):
        if low + SP < TOTAL:
            issue(m + SP, low + SP, min(high + SP, TOTAL))

    def arrive(m, rows=D):
        slot = lax.rem(m, SP)
        for half in range(2):
            dst = wbuf.at[slot, half, pl.ds(0, rows)]
            pltpu.make_async_copy(dst, dst, wsem.at[slot, half]).wait()
        return slot

    def remote(src, dst, send, recv, to):
        return pltpu.make_async_remote_copy(src_ref=src, dst_ref=dst, send_sem=send, recv_sem=recv,
                                            device_id={'tp': to}, device_id_type=MESH)

    own_rows = pltpu.make_async_copy(hid.at[0], hx.at[d], lsem.at[0])
    own_rows.start()
    own_pos = pltpu.make_async_copy(pos, posb.at[d], lsem.at[1])
    own_pos.start()
    own_mask = pltpu.make_async_copy(tmask.at[0], maskb.at[d], lsem.at[2])
    own_mask.start()
    own_vis = pltpu.make_async_copy(vis.at[0], vg.at[d], lsem.at[3])
    own_vis.start()
    for m in range(SP):
        issue(m, m, m + 1)

    barrier = pltpu.get_barrier_semaphore()
    for peer in peers:
        pl.semaphore_signal(barrier, inc=1, device_id={'tp': peer}, device_id_type=MESH)
    pl.semaphore_wait(barrier, 3)

    own_rows.wait()
    own_pos.wait()
    own_mask.wait()
    first_sends = []
    for k, peer in enumerate(peers):
        first_sends.append(remote(hx.at[d], hx.at[d], hs.at[k], hr.at[k], peer))
        first_sends.append(remote(posb.at[d], posb.at[d], ps.at[k], pr.at[k], peer))
        first_sends.append(remote(maskb.at[d], maskb.at[d], ms.at[k], mr.at[k], peer))
    for copy in first_sends:
        copy.start()
    own_vis.wait()
    vis_part = remote(vg.at[d], vg.at[d], vs.at[0], vr.at[0], part)
    vis_part.start()

    def vis_half(block, n, index, to):
        rows = pl.ds(n * (VB // 2), VB // 2)
        return remote(vg.at[block, rows], vg.at[block, rows], vs.at[index], vr.at[index], to)

    vis_half(d, 0, 1, cross).start()

    for k, peer in enumerate(peers):
        remote(posb.at[peer], posb.at[peer], ps.at[k], pr.at[k], peer).wait_recv()
        remote(maskb.at[peer], maskb.at[peer], ms.at[k], mr.at[k], peer).wait_recv()

    lane = lax.broadcasted_iota(jnp.int32, (TB, HD), 1)
    sign = jnp.where(lane < HD // 2, -1.0, 1.0)
    eye = lax.broadcasted_iota(jnp.int32, (TB, TB), 0) == lax.broadcasted_iota(jnp.int32, (TB, TB), 1)
    freqs = freq[...]
    for block in range(4):
        row = posb[block].astype(F32)
        column = jnp.sum(jnp.where(eye, jnp.broadcast_to(row, (TB, TB)), 0.0), axis=1, keepdims=True)
        angles = column * freqs
        cosb[pl.ds(block * TB, TB), :] = jnp.cos(angles)
        sinb[pl.ds(block * TB, TB), :] = jnp.sin(angles) * sign

    for k, peer in enumerate(peers):
        remote(hx.at[peer], hx.at[peer], hs.at[k], hr.at[k], peer).wait_recv()

    for c in range(D // NC):
        h[c] = hx[:, :, c * NC:(c + 1) * NC].reshape(T, NC)

    def normalise(gain):
        total = jnp.zeros((T, NC), F32)
        for c in range(D // NC):
            v = h[c].astype(F32)
            total = total + v * v
        scale = lax.rsqrt(jnp.sum(total, axis=1, keepdims=True) * (1.0 / D) + NORM_EPS)
        for c in range(D // NC):
            g = gain[pl.ds(c * NC, NC)].astype(F32).reshape(1, NC)
            x[:, c * NC:(c + 1) * NC] = (h[c].astype(F32) * scale * g).astype(BF16)

    def head_norm(v, gain):
        scale = lax.rsqrt(jnp.mean(v * v, axis=1, keepdims=True) + NORM_EPS)
        return v * scale * gain[...].astype(F32).reshape(1, HD)

    def rope(v):
        return v * cosb[...] + pltpu.roll(v, HD // 2, 1) * sinb[...]

    def project(m, lhs):
        slot = arrive(m)
        return dot(lhs, wbuf[slot, 0]), dot(lhs, wbuf[slot, 1])

    def attend(keys, mask):
        for g in range(KV):
            q = qb[pl.ds(g * REP, REP)].reshape(REP * T, HD)
            scores = dot_t(q, kb[g, pl.ds(0, keys)]) * (HD ** -0.5)
            scores = jnp.where(mask, scores, MASK_VALUE)
            top = jnp.max(scores, axis=1, keepdims=True)
            e = jnp.exp(scores - top)
            p = (e / jnp.sum(e, axis=1, keepdims=True)).astype(BF16)
            o = dot(p, vb[g, pl.ds(0, keys)]).astype(BF16)
            for r in range(REP):
                head = g * REP + r
                ctx[:, head * HD:(head + 1) * HD] = o[r * T:(r + 1) * T]

    def reduce_all(parity, lag1, lag2, partials, update):
        def step(j, carry):
            @pl.when(j < 8)
            def _():
                low, high = partials(j)
                pb[0, j] = low.astype(BF16)
                pb[1, j] = high.astype(BF16)
                remote(pb.at[1 - core, j], rcv1.at[j], s1.at[j], r1.at[j], part).start()

            @pl.when(jnp.logical_and(j >= lag1, j < 8 + lag1))
            def _():
                i = j - lag1
                remote(pb.at[1 - core, i], rcv1.at[i], s1.at[i], r1.at[i], part).wait_recv()
                snd2[i] = (pb[core, i].astype(F32) + rcv1[i].astype(F32)).astype(BF16)
                remote(snd2.at[i], rcv2.at[parity, i], s2.at[parity, i], r2.at[parity, i], cross).start()

            @pl.when(j >= lag2)
            def _():
                i = j - lag2
                remote(snd2.at[i], rcv2.at[parity, i], s2.at[parity, i], r2.at[parity, i], cross).wait_recv()
                total = snd2[i].astype(F32) + rcv2[parity, i].astype(F32)
                mine = core * 8 + i
                h[mine] = (h[mine].astype(F32) + update(total)).astype(BF16)
                remote(h.at[mine], h.at[mine], s3.at[i], r3.at[i], part).start()
            return carry

        lax.fori_loop(0, 8 + lag2, step, 0)

        def finish(i, carry):
            theirs = (1 - core) * 8 + i
            mine = core * 8 + i
            remote(h.at[theirs], h.at[theirs], s3.at[i], r3.at[i], part).wait_recv()
            remote(h.at[mine], h.at[mine], s3.at[i], r3.at[i], part).wait_send()
            remote(pb.at[1 - core, i], rcv1.at[i], s1.at[i], r1.at[i], part).wait_send()
            remote(snd2.at[i], rcv2.at[parity, i], s2.at[parity, i], r2.at[parity, i], cross).wait_send()
            return carry

        return finish

    def wo_partials(base):
        def partials(j):
            m = base + j // 4
            sub = lax.rem(j, 4)
            slot = lax.rem(m, SP)

            @pl.when(sub == 0)
            def _():
                arrive(m)
            rows = pl.ds(pl.multiple_of(sub * WO_ROWS, WO_ROWS), WO_ROWS)
            low = dot(ctx[...], wbuf[slot, 0, rows])
            high = dot(ctx[...], wbuf[slot, 1, rows])

            @pl.when(sub == 3)
            def _():
                refill(m, base, base + 2)
            return low, high
        return partials

    def wd_partials(base):
        def partials(j):
            m = base + j
            slot = arrive(m, FF)
            rows = pl.ds(0, FF)
            low = dot(act[...], wbuf[slot, 0, rows])
            high = dot(act[...], wbuf[slot, 1, rows])
            refill(m, base, base + 8)
            return low, high
        return partials

    def mlp_up(base):
        def step(i, carry):
            m = base + i
            gate, up = project(m, x[...])
            act[:, cols(i)] = (gate * jax.nn.sigmoid(gate) * up).astype(BF16)
            refill(m, base, base + 14)
            return carry
        lax.fori_loop(0, 14, step, 0)

    normalise(ln1a)

    def q_step_a(i, carry):
        m = BASE['qa'] + i
        for half, q in enumerate(project(m, x[...])):
            for sub in range(2):
                qb[4 * i + 2 * half + sub] = rope(q[:, sub * HD:(sub + 1) * HD]).astype(BF16)
        refill(m, BASE['qa'], BASE['qa'] + 2)
        return carry

    lax.fori_loop(0, 2, q_step_a, 0)
    keys, vals = project(BASE['kva'], x[...])
    for g in range(KV):
        kb[g, pl.ds(0, T)] = rope(keys[:, g * HD:(g + 1) * HD]).astype(BF16)
        vb[g, pl.ds(0, T)] = vals[:, g * HD:(g + 1) * HD].astype(BF16)
    refill(BASE['kva'], BASE['kva'], BASE['kva'] + 1)
    query_at = lax.rem(lax.broadcasted_iota(jnp.int32, (REP * T, T), 0), T)
    attend(T, query_at >= lax.broadcasted_iota(jnp.int32, (REP * T, T), 1))
    lax.fori_loop(0, 8, reduce_all(0, 3, 7, wo_partials(BASE['oa']), lambda total: total), 0)
    vis_half(d, 1, 2, cross).start()
    normalise(ln2a)
    mlp_up(BASE['gua'])
    for n in range(2):
        vis_half(cross, n, 1 + n, cross).wait_recv()
        vis_half(cross, n, 3 + n, part).start()
    end_a = reduce_all(1, 1, 4, wd_partials(BASE['da']), lambda total: total)

    remote(vg.at[part], vg.at[part], vs.at[0], vr.at[0], part).wait_recv()
    for n in range(2):
        vis_half(diag, n, 3 + n, part).wait_recv()
    slot_kv = arrive(BASE['kvb'])

    def kv_step(block, carry):
        rows = pl.ds(pl.multiple_of(block * VB, VB), VB)
        keys = dot(vg[block], wbuf[slot_kv, 0])
        vals = dot(vg[block], wbuf[slot_kv, 1])
        for g in range(KV):
            kb[g, rows] = head_norm(keys[:, g * HD:(g + 1) * HD], kn).astype(BF16)
            vb[g, rows] = vals[:, g * HD:(g + 1) * HD].astype(BF16)
        return carry

    lax.fori_loop(0, 4, kv_step, 0)
    refill(BASE['kvb'], BASE['kvb'], BASE['kvb'] + 1)
    lax.fori_loop(0, 8, end_a, 0)
    normalise(ln1b)

    def q_step_b(i, carry):
        m = BASE['qb'] + i
        for half, q in enumerate(project(m, x[...])):
            for sub in range(2):
                qb[4 * i + 2 * half + sub] = head_norm(q[:, sub * HD:(sub + 1) * HD], qn).astype(BF16)
        refill(m, BASE['qb'], BASE['qb'] + 2)
        return carry

    lax.fori_loop(0, 2, q_step_b, 0)
    seen = (maskb[...].reshape(T, 4) > 0).astype(F32)
    tile_at = lax.broadcasted_iota(jnp.int32, (T, V), 1) // (V // 4)
    visible = jnp.zeros((T, V), F32)
    for tile in range(4):
        visible = jnp.where(tile_at == tile, jnp.broadcast_to(seen[:, tile:tile + 1], (T, V)), visible)
    attend(V, jnp.concatenate([visible] * REP, axis=0) > 0.0)
    keep = jnp.max(seen, axis=1, keepdims=True)
    gate0 = jnp.tanh(jnp.full((T, 1), xg[0], F32)) * keep
    lax.fori_loop(0, 8, reduce_all(2, 3, 7, wo_partials(BASE['ob']), lambda total: gate0 * total), 0)
    normalise(ln2b)
    mlp_up(BASE['gub'])

    own_seen = (maskb[d] > 0).astype(F32)
    gate1 = jnp.tanh(jnp.full((TB, 1), xg[1], F32)) * jnp.max(own_seen, axis=1, keepdims=True)
    down = wd_partials(BASE['db'])
    lag = 3

    def last_step(j, carry):
        @pl.when(j < 8)
        def _():
            for half, value in enumerate(down(j)):
                pf[j, :, half] = value.astype(BF16).reshape(4, TB, NC)
            for k, peer in enumerate(peers):
                remote(pf.at[j, peer], rcvf.at[j, k], fs.at[j, k], fr.at[j, k], peer).start()

        @pl.when(j >= lag)
        def _():
            i = j - lag
            for k, peer in enumerate(peers):
                remote(pf.at[i, peer], rcvf.at[i, k], fs.at[i, k], fr.at[i, k], peer).wait_recv()
            for half in range(2):
                total = pf[i, d, half].astype(F32)
                for k in range(3):
                    total = total + rcvf[i, k, half].astype(F32)
                chunk = i + 8 * half
                rows = pl.ds(pl.multiple_of(d * TB, TB), TB)
                out[0, :, cols(chunk)] = (h[chunk, rows].astype(F32) + gate1 * total).astype(BF16)
        return carry

    lax.fori_loop(0, 8 + lag, last_step, 0)

    for copy in first_sends:
        copy.wait_send()
    vis_part.wait_send()
    for n in range(2):
        vis_half(d, n, 1 + n, cross).wait_send()
        vis_half(cross, n, 3 + n, part).wait_send()

    def drain(j, carry):
        for k, peer in enumerate(peers):
            remote(pf.at[j, peer], rcvf.at[j, k], fs.at[j, k], fr.at[j, k], peer).wait_send()
        return carry

    lax.fori_loop(0, 8, drain, 0)


def solution(mesh):
    act_spec = P('dp', 'tp', None)
    col_spec = P(None, 'tp')
    row_spec = P('tp', None)
    layer_a = (P(), col_spec, col_spec, col_spec, row_spec, P(), col_spec, col_spec, row_spec)
    layer_b = (P(), col_spec, P(), col_spec, col_spec, P(), row_spec, P(), col_spec, col_spec, row_spec, P())
    in_specs = (act_spec, act_spec, P('dp', 'tp'), act_spec) + layer_a + layer_b
    table = rope_table(HD)

    hbm = pl.BlockSpec(memory_space=pl.ANY)
    vmem = pl.BlockSpec(memory_space=pltpu.VMEM)
    smem = pl.BlockSpec(memory_space=pltpu.SMEM)
    dma = pltpu.SemaphoreType.DMA
    scratch = [
        pltpu.VMEM((SP, 2, D, NC), BF16), dma((SP, 2)),
        pltpu.VMEM((4, TB, D), BF16),
        pltpu.VMEM((4, 1, TB), jnp.int32),
        pltpu.VMEM((4, TB, 4), jnp.int32),
        pltpu.VMEM((T, HD), F32), pltpu.VMEM((T, HD), F32),
        pltpu.VMEM((D // NC, T, NC), BF16),
        pltpu.VMEM((T, D), BF16),
        pltpu.VMEM((T, FF), BF16),
        pltpu.VMEM((T, WO_ROWS), BF16),
        pltpu.VMEM((KV * REP, T, HD), BF16),
        pltpu.VMEM((KV, V, HD), BF16), pltpu.VMEM((KV, V, HD), BF16),
        pltpu.VMEM((4, VB, D), BF16),
        pltpu.VMEM((2, 8, T, NC), BF16),
        pltpu.VMEM((8, T, NC), BF16),
        pltpu.VMEM((8, T, NC), BF16),
        pltpu.VMEM((3, 8, T, NC), BF16),
        pltpu.VMEM((8, 4, 2, TB, NC), BF16),
        pltpu.VMEM((8, 3, 2, TB, NC), BF16),
        dma((4,)),
        dma((3,)), dma((3,)), dma((3,)), dma((3,)), dma((3,)), dma((3,)),
        dma((5,)), dma((5,)),
        dma((8,)), dma((8,)), dma((3, 8)), dma((3, 8)), dma((8,)), dma((8,)),
        dma((8, 3)), dma((8, 3)),
    ]

    def body(hidden, vision, positions, tile_mask, *params):
        freqs = jnp.asarray(np.concatenate([table, table])[None])
        specs = [hbm, hbm, hbm, hbm, vmem]
        for k, p in enumerate(params):
            specs.append(vmem if p.ndim == 1 else hbm)
        specs[-1] = smem
        return pl.pallas_call(
            kernel,
            out_shape=jax.ShapeDtypeStruct(hidden.shape, BF16),
            in_specs=specs,
            out_specs=vmem,
            scratch_shapes=scratch,
            compiler_params=pltpu.CompilerParams(
                collective_id=0, has_side_effects=True, vmem_limit_bytes=67043328),
            cost_estimate=pl.CostEstimate(flops=2 * 64 * 109051904, bytes_accessed=218103808, transcendentals=0),
            name='layers',
        )(hidden, vision, positions, tile_mask, freqs, *params)

    return jax.shard_map(body, mesh=mesh, in_specs=in_specs, out_specs=act_spec, check_vma=False)
```

time: 263 us -> 109 us (0.41)
  Pallas kernels: 0 us -> 106 us
  matrix products: 99 us -> 0 us
  blocking collectives: 57.6 us -> 0 us
  waiting for transfers between devices: 48.4 us -> 0 us
  local copies, waits for them, and re-layouts: 31.5 us -> 2.92 us
  between operations: 14.2 us -> 0.01 us
  other arithmetic: 11.1 us -> 0 us
    pallas_call x0 -> x1, Pallas kernels: none -> 106 us  [body(): pl.pallas_call(kernel, out_shape=jax.ShapeDtypeStruct(hidden.shape, BF16)...]
    dot_general x12 -> x0, matrix products: 96 us -> none  [the longest x2 45.5 us: gated_mlp(): jnp.einsum('btf,fd->btd', activated, w_down, preferred_element_type=jnp.f...]
    all_gather x5 -> x0, blocking collectives: 53 us -> none  [gather_rows(): return lax.all_gather(values, 'tp', axis=1, tiled=True)]
    reduce_scatter x4 -> x0, waiting for transfers between devices: 47.6 us -> none  [scatter_sum(): lax.psum_scatter(partial, 'tp', scatter_dimension=1, tiled=True)]
    reshape x2 -> x0, local copies, waits for them, and re-layouts: 28.6 us -> none  [the longest x1 14.3 us: body(): wq_b.reshape(query_shape)]
    convert_element_type x12 -> x0, other arithmetic: 4.81 us -> none  [the longest x1 1.73 us: body(): (h_three.astype(jnp.float32) + gate_vals[1] * row_keep * mlp_out).astype(...]
    unnamed x1 -> x0, blocking collectives: 4.55 us -> none
    reduce_sum x4 -> x0, other arithmetic: 4.3 us -> none  [rms_scale(): mean_sq = jnp.mean(values * values, axis=-1, keepdims=True)]
  transfers between devices with their start and end apart: 5 -> 0, of which waited for: 3 -> 0; matrix products, arithmetic and copies ran while one was open for 9% -> 0% of each run, Pallas kernels for 0% -> 0%
where the time goes in v1:
time: 109 us
  Pallas kernels  106 us (97%)
  local copies, waits for them, and re-layouts  2.92 us (3%)
    pallas_call x1, Pallas kernels, body(): pl.pallas_call(kernel, out_shape=jax.ShapeDtypeStruct(hidden.shape, BF16)...  106 us
    unnamed x2, local copies, waits for them, and re-layouts  2.92 us

profile of v1, /device:TPU:0, one launch (start us, length us, event | category | flops | bytes accessed | tf_op | source)
XLA Modules:
  0.0 109.1 jit_solution(16025426857101607358)
XLA Ops:
  0.0 1.4 %copy.27.tmask = s32[1,16,4]{2,1,0:T(8,128)} copy(s32[1,16,4]{1,2,0:T(4,128)} %param.29) | data formatting | bytes 512 | tf_op args[3]
  1.4 106.2 %layers.1 = bf16[1,16,4096]{2,1,0:T(8,128)(2,1)} custom-call(bf16[1,16,4096]{2,1,0:T(8,128)(2,1)} %hid.1, bf16[1,64,4096]{2,1,0:T(8,128)(2,1)} %vis.1, s32[1,16]{1,0:T(1,128)} %pos.1, s32[1,16,4]{2,1,0:T(8,128)} %copy.27.tmask, f32[1,128]{1,0:T(1,128)} %constant.2.clone.freq, bf16[4096]{0:T(1024)(128)(2,1)} %ln1a.1, bf16[4096,1024]{1,0:T(8,128)(2,1)} %wqa.1, ...), custom_call_target="tpu_custom_call" | custom-call | flops 13958643712 | bytes 218103808 | tf_op jit(solution)/shard_map/layers/pallas_call | solution.py:464
  107.6 1.6 %copy.29 = bf16[1,16,4096]{2,1,0:T(8,128)(2,1)} copy(bf16[1,16,4096]{2,1,0:T(8,128)(2,1)} %layers.1) | data formatting | bytes 262144

commit v2 on v1

v2 whole, which is shorter than its diff:
```python
import math
import jax
import jax.numpy as jnp
import numpy as np
from jax import lax
from jax.experimental import pallas as pl
from jax.experimental.pallas import tpu as pltpu
from jax.sharding import PartitionSpec as P

ROPE_THETA = 500000.0
ROPE_FACTOR = 8.0
LOW_FACTOR = 1.0
HIGH_FACTOR = 4.0
ORIG_CONTEXT = 8192.0
NORM_EPS = 1e-5
MASK_VALUE = -1e30
MESH = pl.DeviceIdType.MESH
BF16 = jnp.bfloat16
F32 = jnp.float32

T = 64
TB = 16
D = 4096
V = 256
VB = 64
HD = 128
KV = 2
REP = 4
FF = 3584
NC = 256
SP = 13
WO_ROWS = KV * REP * HD

SEGMENTS = []
_at = 0
for _name, _count in (('qa', 2), ('kva', 1), ('oa', 2), ('gua', 14), ('da', 8),
                      ('kvb', 1), ('qb', 2), ('ob', 2), ('gub', 14), ('db', 8)):
    SEGMENTS.append((_name, _at, _count))
    _at += _count
TOTAL = _at
BASE = {name: first for name, first, _ in SEGMENTS}


def rope_table(head_dim):
    low_wave = ORIG_CONTEXT / LOW_FACTOR
    high_wave = ORIG_CONTEXT / HIGH_FACTOR
    freq_list = []
    for freq_idx in range(head_dim // 2):
        base_freq = 1.0 / (ROPE_THETA ** (2.0 * freq_idx / head_dim))
        wave_len = 2.0 * math.pi / base_freq
        if wave_len > low_wave:
            freq_list.append(base_freq / ROPE_FACTOR)
        elif wave_len < high_wave:
            freq_list.append(base_freq)
        else:
            smooth = (ORIG_CONTEXT / wave_len - LOW_FACTOR) / (HIGH_FACTOR - LOW_FACTOR)
            freq_list.append((1.0 - smooth) * base_freq / ROPE_FACTOR + smooth * base_freq)
    return np.array(freq_list, dtype=np.float32)


def dot(a, b):
    return jnp.dot(a, b, preferred_element_type=F32)


def dot_t(a, b):
    return lax.dot_general(a, b, (((1,), (1,)), ((), ())), preferred_element_type=F32)


def kernel(hid, vis, pos, tmask, freq,
           ln1a, wqa, wka, wva, woa, ln2a, wga, wua, wda,
           ln1b, wqb, qn, wkb, wvb, kn, wob, ln2b, wgb, wub, wdb, xg,
           out,
           wbuf, wsem, hx, posb, maskb, cosb, sinb, visb, keepb, h, x, act, ctx, qb, kb, vb, vg,
           pb, rcv1, snd2, rcv2, pf, rcvf,
           lsem, hs, hr, ps, pr, ms, mr, vs, vr, s1, r1, s2, r2, s3, r3, fs, fr):
    d = lax.axis_index('tp')
    core = lax.rem(d, 2)
    part = d + 1 - 2 * core
    cross = lax.rem(d + 2, 4)
    diag = 3 - d
    peers = (part, cross, diag)
    weights = {
        'qa': (wqa,), 'kva': (wka, wva), 'oa': (woa,), 'gua': (wga, wua), 'da': (wda,),
        'qb': (wqb,), 'kvb': (wkb, wvb), 'ob': (wob,), 'gub': (wgb, wub), 'db': (wdb,),
    }

    def cols(index):
        return pl.ds(pl.multiple_of(index * NC, NC), NC)

    def start_segment(name, first, m):
        slot = lax.rem(m, SP)
        i = m - first
        refs = weights[name]
        kind = name[:-1]
        if kind == 'q':
            for half in range(2):
                pltpu.make_async_copy(refs[0].at[:, cols(2 * i + half)], wbuf.at[slot, half], wsem.at[slot, half]).start()
        elif kind == 'kv':
            for half in range(2):
                pltpu.make_async_copy(refs[half], wbuf.at[slot, half], wsem.at[slot, half]).start()
        elif kind == 'gu':
            for half in range(2):
                pltpu.make_async_copy(refs[half].at[:, cols(i)], wbuf.at[slot, half], wsem.at[slot, half]).start()
        elif kind == 'd':
            for half in range(2):
                pltpu.make_async_copy(refs[0].at[:, cols(i + 8 * half)], wbuf.at[slot, half, pl.ds(0, FF)], wsem.at[slot, half]).start()
        else:
            for half in range(2):
                for sub in range(4):
                    pltpu.make_async_copy(refs[0].at[:, cols(4 * i + sub + 8 * half)],
                                          wbuf.at[slot, half, pl.ds(sub * WO_ROWS, WO_ROWS)], wsem.at[slot, half]).start()

    def issue(m, low, high):
        for name, first, count in SEGMENTS:
            if first >= high or first + count <= low:
                continue
            if first <= low and high <= first + count:
                start_segment(name, first, m)
            else:
                @pl.when(jnp.logical_and(m >= first, m < first + count))
                def _():
                    start_segment(name, first, m)

    def refill(m, low, high):
        if low + SP < TOTAL:
            issue(m + SP, low + SP, high + SP)

    def arrive(m, rows=D):
        slot = lax.rem(m, SP)
        for half in range(2):
            dst = wbuf.at[slot, half, pl.ds(0, rows)]
            pltpu.make_async_copy(dst, dst, wsem.at[slot, half]).wait()
        return slot

    def remote(src, dst, send, recv, to):
        return pltpu.make_async_remote_copy(src_ref=src, dst_ref=dst, send_sem=send, recv_sem=recv,
                                            device_id={'tp': to}, device_id_type=MESH)

    own_rows = pltpu.make_async_copy(hid.at[0], hx.at[d], lsem.at[0])
    own_rows.start()
    own_pos = pltpu.make_async_copy(pos, posb.at[d], lsem.at[1])
    own_pos.start()
    own_mask = pltpu.make_async_copy(tmask.at[0], maskb.at[d], lsem.at[2])
    own_mask.start()
    barrier = pltpu.get_barrier_semaphore()
    for peer in peers:
        pl.semaphore_signal(barrier, inc=1, device_id={'tp': peer}, device_id_type=MESH)
    for m in range(4):
        issue(m, m, m + 1)
    own_vis = pltpu.make_async_copy(vis.at[0], vg.at[d], lsem.at[3])
    own_vis.start()
    for m in range(4, SP):
        issue(m, m, m + 1)
    own_rows.wait()
    own_pos.wait()
    own_mask.wait()
    pl.semaphore_wait(barrier, 3)

    def hid_half(block, n, index, to):
        rows = pl.ds(n * (TB // 2), TB // 2)
        return remote(hx.at[block, rows], hx.at[block, rows], hs.at[index], hr.at[index], to)

    def vis_half(block, n, index, to):
        rows = pl.ds(n * (VB // 2), VB // 2)
        return remote(vg.at[block, rows], vg.at[block, rows], vs.at[index], vr.at[index], to)

    first_sends = [hid_half(d, 0, 1, cross), hid_half(d, 1, 2, cross), remote(hx.at[d], hx.at[d], hs.at[0], hr.at[0], part)]
    for k, peer in enumerate(peers):
        first_sends.append(remote(posb.at[d], posb.at[d], ps.at[k], pr.at[k], peer))
        first_sends.append(remote(maskb.at[d], maskb.at[d], ms.at[k], mr.at[k], peer))
    for copy in first_sends:
        copy.start()
    own_vis.wait()
    vis_part = remote(vg.at[d], vg.at[d], vs.at[0], vr.at[0], part)
    vis_part.start()
    vis_half(d, 0, 1, cross).start()

    for k, peer in enumerate(peers):
        remote(posb.at[peer], posb.at[peer], ps.at[k], pr.at[k], peer).wait_recv()
        remote(maskb.at[peer], maskb.at[peer], ms.at[k], mr.at[k], peer).wait_recv()

    sign = jnp.where(lax.broadcasted_iota(jnp.int32, (TB, HD), 1) < HD // 2, -1.0, 1.0)
    eye = lax.broadcasted_iota(jnp.int32, (TB, TB), 0) == lax.broadcasted_iota(jnp.int32, (TB, TB), 1)
    freqs = freq[...]

    def as_column(row):
        return jnp.sum(jnp.where(eye, jnp.broadcast_to(row, (TB, TB)), 0.0), axis=1, keepdims=True)

    for block in range(4):
        rows = pl.ds(block * TB, TB)
        angles = as_column(posb[block].astype(F32)) * freqs
        cosb[rows, :] = jnp.cos(angles)
        sinb[rows, :] = jnp.sin(angles) * sign
        seen = (maskb[block] > 0).astype(F32)
        for tile in range(4):
            visb[rows, tile * (V // 4):(tile + 1) * (V // 4)] = jnp.broadcast_to(as_column(seen[tile:tile + 1]), (TB, V // 4))
        keepb[rows, :] = jnp.broadcast_to(as_column(jnp.max(seen, axis=0, keepdims=True)), (TB, HD))

    for n in range(2):
        hid_half(cross, n, 1 + n, cross).wait_recv()
        hid_half(cross, n, 3 + n, part).start()
    remote(hx.at[part], hx.at[part], hs.at[0], hr.at[0], part).wait_recv()
    for n in range(2):
        hid_half(diag, n, 3 + n, part).wait_recv()

    for c in range(D // NC):
        h[c] = hx[:, :, c * NC:(c + 1) * NC].reshape(T, NC)

    def normalise(gain):
        total = jnp.zeros((T, NC), F32)
        for c in range(D // NC):
            v = h[c].astype(F32)
            total = total + v * v
        scale = lax.rsqrt(jnp.sum(total, axis=1, keepdims=True) * (1.0 / D) + NORM_EPS)
        for c in range(D // NC):
            g = gain[pl.ds(c * NC, NC)].astype(F32).reshape(1, NC)
            x[:, c * NC:(c + 1) * NC] = (h[c].astype(F32) * scale * g).astype(BF16)

    def head_norm(v, gain):
        scale = lax.rsqrt(jnp.mean(v * v, axis=1, keepdims=True) + NORM_EPS)
        return v * scale * gain[...].astype(F32).reshape(1, HD)

    def rope(v):
        return v * cosb[...] + pltpu.roll(v, HD // 2, 1) * sinb[...]

    def attend(keys, mask):
        for g in range(KV):
            q = qb[pl.ds(g * REP, REP)].reshape(REP * T, HD)
            scores = dot_t(q, kb[g, pl.ds(0, keys)]) * (HD ** -0.5)
            scores = jnp.where(mask, scores, MASK_VALUE)
            top = jnp.max(scores, axis=1, keepdims=True)
            e = jnp.exp(scores - top)
            p = (e / jnp.sum(e, axis=1, keepdims=True)).astype(BF16)
            o = dot(p, vb[g, pl.ds(0, keys)]).astype(BF16)
            for r in range(REP):
                head = g * REP + r
                ctx[:, head * HD:(head + 1) * HD] = o[r * T:(r + 1) * T]

    def spread(parity, partials, update, between=None):
        def hop1(i):
            return remote(pb.at[1 - core, i], rcv1.at[i], s1.at[i], r1.at[i], part)

        def hop2(i):
            return remote(snd2.at[i], rcv2.at[parity, i], s2.at[parity, i], r2.at[parity, i], cross)

        def hop3(half, i):
            return remote(h.at[half * 8 + i], h.at[half * 8 + i], s3.at[i], r3.at[i], part)

        def fold(i):
            hop1(i).wait_recv()
            snd2[i] = (pb[core, i].astype(F32) + rcv1[i].astype(F32)).astype(BF16)
            hop2(i).start()

        def step(j, carry):
            for n, (low, high) in enumerate(partials(j)):
                i = 2 * j + n
                pb[0, i] = low.astype(BF16)
                pb[1, i] = high.astype(BF16)
                hop1(i).start()

            @pl.when(j >= 1)
            def _():
                fold(2 * j - 2)
                fold(2 * j - 1)
            return carry

        lax.fori_loop(0, 4, step, 0)
        fold(6)
        fold(7)
        if between is not None:
            between()

        def final(i, carry):
            hop2(i).wait_recv()
            total = snd2[i].astype(F32) + rcv2[parity, i].astype(F32)
            mine = core * 8 + i
            h[mine] = (h[mine].astype(F32) + update(total)).astype(BF16)
            hop3(core, i).start()
            return carry

        lax.fori_loop(0, 8, final, 0)

        def finish(i, carry):
            hop3(1 - core, i).wait_recv()
            hop3(core, i).wait_send()
            hop1(i).wait_send()
            hop2(i).wait_send()
            return carry

        lax.fori_loop(0, 8, finish, 0)

    def wo_partials(base):
        def partials(j):
            m = base + j // 2
            slot = lax.rem(m, SP)

            @pl.when(lax.rem(j, 2) == 0)
            def _():
                arrive(m)
            out = []
            for n in range(2):
                rows = pl.ds(pl.multiple_of((lax.rem(j, 2) * 2 + n) * WO_ROWS, WO_ROWS), WO_ROWS)
                out.append((dot(ctx[...], wbuf[slot, 0, rows]), dot(ctx[...], wbuf[slot, 1, rows])))

            @pl.when(lax.rem(j, 2) == 1)
            def _():
                refill(m, base, base + 2)
            return out
        return partials

    def wd_partials(base):
        def partials(j):
            slots = [arrive(base + 2 * j + n, FF) for n in range(2)]
            out = []
            for slot in slots:
                rows = pl.ds(0, FF)
                out.append((dot(act[...], wbuf[slot, 0, rows]), dot(act[...], wbuf[slot, 1, rows])))
            for n in range(2):
                refill(base + 2 * j + n, base, base + 8)
            return out
        return partials

    def mlp_up(base):
        def step(i, carry):
            slots = [arrive(base + 2 * i + n) for n in range(2)]
            for n, slot in enumerate(slots):
                gate = dot(x[...], wbuf[slot, 0])
                up = dot(x[...], wbuf[slot, 1])
                act[:, cols(2 * i + n)] = (gate * jax.nn.sigmoid(gate) * up).astype(BF16)
            for n in range(2):
                refill(base + 2 * i + n, base, base + 14)
            return carry
        lax.fori_loop(0, 7, step, 0)

    def queries(base, finish):
        slots = [arrive(base + i) for i in range(2)]
        for i, slot in enumerate(slots):
            for half in range(2):
                q = dot(x[...], wbuf[slot, half])
                for sub in range(2):
                    qb[4 * i + 2 * half + sub] = finish(q[:, sub * HD:(sub + 1) * HD]).astype(BF16)

    normalise(ln1a)
    slot_kv = arrive(BASE['kva'])
    queries(BASE['qa'], rope)
    keys, vals = dot(x[...], wbuf[slot_kv, 0]), dot(x[...], wbuf[slot_kv, 1])
    for g in range(KV):
        kb[g, pl.ds(0, T)] = rope(keys[:, g * HD:(g + 1) * HD]).astype(BF16)
        vb[g, pl.ds(0, T)] = vals[:, g * HD:(g + 1) * HD].astype(BF16)
    for m in range(3):
        refill(m, m, m + 1)
    query_at = lax.rem(lax.broadcasted_iota(jnp.int32, (REP * T, T), 0), T)
    attend(T, query_at >= lax.broadcasted_iota(jnp.int32, (REP * T, T), 1))
    spread(0, wo_partials(BASE['oa']), lambda total: total)
    vis_half(d, 1, 2, cross).start()
    normalise(ln2a)
    mlp_up(BASE['gua'])
    for n in range(2):
        vis_half(cross, n, 1 + n, cross).wait_recv()
        vis_half(cross, n, 3 + n, part).start()

    def vision_heads():
        remote(vg.at[part], vg.at[part], vs.at[0], vr.at[0], part).wait_recv()
        for n in range(2):
            vis_half(diag, n, 3 + n, part).wait_recv()
        slot = arrive(BASE['kvb'])

        def kv_step(n, carry):
            rows = pl.ds(pl.multiple_of(n * 2 * VB, 2 * VB), 2 * VB)
            lhs = vg[pl.ds(2 * n, 2)].reshape(2 * VB, D)
            keys = dot(lhs, wbuf[slot, 0])
            vals = dot(lhs, wbuf[slot, 1])
            for g in range(KV):
                kb[g, rows] = head_norm(keys[:, g * HD:(g + 1) * HD], kn).astype(BF16)
                vb[g, rows] = vals[:, g * HD:(g + 1) * HD].astype(BF16)
            return carry

        lax.fori_loop(0, 2, kv_step, 0)
        refill(BASE['kvb'], BASE['kvb'], BASE['kvb'] + 1)

    spread(1, wd_partials(BASE['da']), lambda total: total, vision_heads)

    normalise(ln1b)
    queries(BASE['qb'], lambda q: head_norm(q, qn))
    for i in range(2):
        refill(BASE['qb'] + i, BASE['qb'] + i, BASE['qb'] + i + 1)
    attend(V, jnp.concatenate([visb[...]] * REP, axis=0) > 0.0)
    gate0 = jnp.tanh(jnp.full((T, 1), xg[0], F32)) * keepb[:, 0:1]
    spread(2, wo_partials(BASE['ob']), lambda total: gate0 * total)
    normalise(ln2b)
    mlp_up(BASE['gub'])

    own = pl.ds(pl.multiple_of(d * TB, TB), TB)
    gate1 = jnp.tanh(jnp.full((TB, 1), xg[1], F32)) * keepb[own, 0:1]
    down = wd_partials(BASE['db'])

    def last_step(j, carry):
        for n, values in enumerate(down(j)):
            i = 2 * j + n
            for half, value in enumerate(values):
                pf[i, :, half] = value.astype(BF16).reshape(4, TB, NC)
            for k, peer in enumerate(peers):
                remote(pf.at[i, peer], rcvf.at[i, k], fs.at[i, k], fr.at[i, k], peer).start()
        return carry

    lax.fori_loop(0, 4, last_step, 0)

    def last_sum(i, carry):
        for k, peer in enumerate(peers):
            remote(pf.at[i, peer], rcvf.at[i, k], fs.at[i, k], fr.at[i, k], peer).wait_recv()
        for half in range(2):
            total = pf[i, d, half].astype(F32)
            for k in range(3):
                total = total + rcvf[i, k, half].astype(F32)
            chunk = i + 8 * half
            out[0, :, cols(chunk)] = (h[chunk, own].astype(F32) + gate1 * total).astype(BF16)
        return carry

    lax.fori_loop(0, 8, last_sum, 0)

    for copy in first_sends:
        copy.wait_send()
    vis_part.wait_send()
    for n in range(2):
        hid_half(cross, n, 3 + n, part).wait_send()
        vis_half(d, n, 1 + n, cross).wait_send()
        vis_half(cross, n, 3 + n, part).wait_send()

    def drain(j, carry):
        for k, peer in enumerate(peers):
            remote(pf.at[j, peer], rcvf.at[j, k], fs.at[j, k], fr.at[j, k], peer).wait_send()
        return carry

    lax.fori_loop(0, 8, drain, 0)


def solution(mesh):
    act_spec = P('dp', 'tp', None)
    col_spec = P(None, 'tp')
    row_spec = P('tp', None)
    layer_a = (P(), col_spec, col_spec, col_spec, row_spec, P(), col_spec, col_spec, row_spec)
    layer_b = (P(), col_spec, P(), col_spec, col_spec, P(), row_spec, P(), col_spec, col_spec, row_spec, P())
    in_specs = (act_spec, act_spec, P('dp', 'tp'), act_spec) + layer_a + layer_b
    table = rope_table(HD)

    hbm = pl.BlockSpec(memory_space=pl.ANY)
    vmem = pl.BlockSpec(memory_space=pltpu.VMEM)
    smem = pl.BlockSpec(memory_space=pltpu.SMEM)
    dma = pltpu.SemaphoreType.DMA
    scratch = [
        pltpu.VMEM((SP, 2, D, NC), BF16), dma((SP, 2)),
        pltpu.VMEM((4, TB, D), BF16),
        pltpu.VMEM((4, 1, TB), jnp.int32),
        pltpu.VMEM((4, 4, TB), jnp.int32),
        pltpu.VMEM((T, HD), F32), pltpu.VMEM((T, HD), F32),
        pltpu.VMEM((T, V), F32), pltpu.VMEM((T, HD), F32),
        pltpu.VMEM((D // NC, T, NC), BF16),
        pltpu.VMEM((T, D), BF16),
        pltpu.VMEM((T, FF), BF16),
        pltpu.VMEM((T, WO_ROWS), BF16),
        pltpu.VMEM((KV * REP, T, HD), BF16),
        pltpu.VMEM((KV, V, HD), BF16), pltpu.VMEM((KV, V, HD), BF16),
        pltpu.VMEM((4, VB, D), BF16),
        pltpu.VMEM((2, 8, T, NC), BF16),
        pltpu.VMEM((8, T, NC), BF16),
        pltpu.VMEM((8, T, NC), BF16),
        pltpu.VMEM((3, 8, T, NC), BF16),
        pltpu.VMEM((8, 4, 2, TB, NC), BF16),
        pltpu.VMEM((8, 3, 2, TB, NC), BF16),
        dma((4,)),
        dma((5,)), dma((5,)), dma((3,)), dma((3,)), dma((3,)), dma((3,)),
        dma((5,)), dma((5,)),
        dma((8,)), dma((8,)), dma((3, 8)), dma((3, 8)), dma((8,)), dma((8,)),
        dma((8, 3)), dma((8, 3)),
    ]

    def body(hidden, vision, positions, tile_mask, *params):
        freqs = jnp.asarray(np.concatenate([table, table])[None])
        specs = [hbm, hbm, hbm, hbm, vmem]
        for k, p in enumerate(params):
            specs.append(vmem if p.ndim == 1 else hbm)
        specs[-1] = smem
        return pl.pallas_call(
            kernel,
            out_shape=jax.ShapeDtypeStruct(hidden.shape, BF16),
            in_specs=specs,
            out_specs=vmem,
            scratch_shapes=scratch,
            compiler_params=pltpu.CompilerParams(
                collective_id=0, has_side_effects=True, vmem_limit_bytes=67043328),
            cost_estimate=pl.CostEstimate(flops=2 * 64 * 109051904, bytes_accessed=218103808, transcendentals=0),
            name='layers',
        )(hidden, vision, positions, jnp.swapaxes(tile_mask, 1, 2), freqs, *params)

    return jax.shard_map(body, mesh=mesh, in_specs=in_specs, out_specs=act_spec, check_vma=False)
```

time: 109 us -> 93.5 us (0.86)
  Pallas kernels: 106 us -> 91.8 us
  local copies, waits for them, and re-layouts: 2.92 us -> 1.57 us
    pallas_call x1, Pallas kernels: 106 us -> 91.8 us  [body(): pl.pallas_call(kernel, out_shape=jax.ShapeDtypeStruct(hidden.shape, BF16)...]
    unnamed x2 -> x1, local copies, waits for them, and re-layouts: 2.92 us -> 1.57 us
where the time goes in v2:
time: 93.5 us; the launch traced here: 93.4 us
  Pallas kernels  91.8 us (98%)
  local copies, waits for them, and re-layouts  1.57 us (2%)
    pallas_call x1, Pallas kernels, body(): pl.pallas_call(kernel, out_shape=jax.ShapeDtypeStruct(hidden.shape, BF16)...  91.8 us

profile of v2, /device:TPU:0, one launch (start us, length us, event | category | flops | bytes accessed | tf_op | source)
XLA Modules:
  0.0 93.4 jit_solution(11311988507541795141)
XLA Ops:
  0.0 91.8 %layers.1 = bf16[1,16,4096]{2,1,0:T(8,128)(2,1)} custom-call(bf16[1,16,4096]{2,1,0:T(8,128)(2,1)} %hid.1, bf16[1,64,4096]{2,1,0:T(8,128)(2,1)} %vis.1, s32[1,16]{1,0:T(1,128)} %pos.1, s32[1,4,16]{2,1,0:T(4,128)} %bitcast.1, f32[1,128]{1,0:T(1,128)} %constant.2.clone.freq, bf16[4096]{0:T(1024)(128)(2,1)} %ln1a.1, bf16[4096,1024]{1,0:T(8,128)(2,1)} %wqa.1, ...), custom_call_target="tpu_custom_call" | custom-call | flops 13958643712 | bytes 218103808 | tf_op jit(solution)/shard_map/layers/pallas_call | solution.py:483
  91.8 1.6 %copy.28 = bf16[1,16,4096]{2,1,0:T(8,128)(2,1)} copy(bf16[1,16,4096]{2,1,0:T(8,128)(2,1)} %layers.1) | data formatting | bytes 262144

commit v3 on v2

--- a/solution.py
+++ b/solution.py
@@ -71,7 +71,7 @@
            ln1b, wqb, qn, wkb, wvb, kn, wob, ln2b, wgb, wub, wdb, xg,
            out,
            wbuf, wsem, hx, posb, maskb, cosb, sinb, visb, keepb, h, x, act, ctx, qb, kb, vb, vg,
-           pb, rcv1, snd2, rcv2, pf, rcvf,
+           pb, rcv1, snd2, rcv2, pf, rcvf, obuf, osem,
            lsem, hs, hr, ps, pr, ms, mr, vs, vr, s1, r1, s2, r2, s3, r3, fs, fr):
     d = lax.axis_index('tp')
     core = lax.rem(d, 2)
@@ -142,14 +142,12 @@
     own_pos.start()
     own_mask = pltpu.make_async_copy(tmask.at[0], maskb.at[d], lsem.at[2])
     own_mask.start()
+    own_vis = pltpu.make_async_copy(vis.at[0], vg.at[d], lsem.at[3])
+    own_vis.start()
     barrier = pltpu.get_barrier_semaphore()
     for peer in peers:
         pl.semaphore_signal(barrier, inc=1, device_id={'tp': peer}, device_id_type=MESH)
     for m in range(4):
-        issue(m, m, m + 1)
-    own_vis = pltpu.make_async_copy(vis.at[0], vg.at[d], lsem.at[3])
-    own_vis.start()
-    for m in range(4, SP):
         issue(m, m, m + 1)
     own_rows.wait()
     own_pos.wait()
@@ -170,10 +168,9 @@
         first_sends.append(remote(maskb.at[d], maskb.at[d], ms.at[k], mr.at[k], peer))
     for copy in first_sends:
         copy.start()
-    own_vis.wait()
+    for m in range(4, SP):
+        issue(m, m, m + 1)
     vis_part = remote(vg.at[d], vg.at[d], vs.at[0], vr.at[0], part)
-    vis_part.start()
-    vis_half(d, 0, 1, cross).start()
 
     for k, peer in enumerate(peers):
         remote(posb.at[peer], posb.at[peer], ps.at[k], pr.at[k], peer).wait_recv()
@@ -196,9 +193,12 @@
             visb[rows, tile * (V // 4):(tile + 1) * (V // 4)] = jnp.broadcast_to(as_column(seen[tile:tile + 1]), (TB, V // 4))
         keepb[rows, :] = jnp.broadcast_to(as_column(jnp.max(seen, axis=0, keepdims=True)), (TB, HD))
 
+    own_vis.wait()
     for n in range(2):
         hid_half(cross, n, 1 + n, cross).wait_recv()
         hid_half(cross, n, 3 + n, part).start()
+    vis_part.start()
+    vis_half(d, 0, 1, cross).start()
     remote(hx.at[part], hx.at[part], hs.at[0], hr.at[0], part).wait_recv()
     for n in range(2):
         hid_half(diag, n, 3 + n, part).wait_recv()
@@ -413,7 +413,8 @@
             for k in range(3):
                 total = total + rcvf[i, k, half].astype(F32)
             chunk = i + 8 * half
-            out[0, :, cols(chunk)] = (h[chunk, own].astype(F32) + gate1 * total).astype(BF16)
+            obuf[:, cols(chunk)] = (h[chunk, own].astype(F32) + gate1 * total).astype(BF16)
+            pltpu.make_async_copy(obuf.at[:, cols(chunk)], out.at[0, :, cols(chunk)], osem.at[i, half]).start()
         return carry
 
     lax.fori_loop(0, 8, last_sum, 0)
@@ -427,6 +428,9 @@
         vis_half(cross, n, 3 + n, part).wait_send()
 
     def drain(j, carry):
+        for half in range(2):
+            piece = cols(j + 8 * half)
+            pltpu.make_async_copy(obuf.at[:, piece], out.at[0, :, piece], osem.at[j, half]).wait()
         for k, peer in enumerate(peers):
             remote(pf.at[j, peer], rcvf.at[j, k], fs.at[j, k], fr.at[j, k], peer).wait_send()
         return carry
@@ -467,6 +471,7 @@
         pltpu.VMEM((3, 8, T, NC), BF16),
         pltpu.VMEM((8, 4, 2, TB, NC), BF16),
         pltpu.VMEM((8, 3, 2, TB, NC), BF16),
+        pltpu.VMEM((TB, D), BF16), dma((8, 2)),
         dma((4,)),
         dma((5,)), dma((5,)), dma((3,)), dma((3,)), dma((3,)), dma((3,)),
         dma((5,)), dma((5,)),
@@ -484,7 +489,7 @@
             kernel,
             out_shape=jax.ShapeDtypeStruct(hidden.shape, BF16),
             in_specs=specs,
-            out_specs=vmem,
+            out_specs=hbm,
             scratch_shapes=scratch,
             compiler_params=pltpu.CompilerParams(
                 collective_id=0, has_side_effects=True, vmem_limit_bytes=67043328),

time: 93.5 us -> 83 us (0.89)
  Pallas kernels: 91.8 us -> 81.2 us
    pallas_call x1, Pallas kernels: 91.8 us -> 81.2 us  [body(): pl.pallas_call(kernel, out_shape=jax.ShapeDtypeStruct(hidden.shape, BF16)...]
where the time goes in v3:
time: 83 us; the launch traced here: 82.8 us
  Pallas kernels  81.2 us (98%)
  local copies, waits for them, and re-layouts  1.57 us (2%)
    pallas_call x1, Pallas kernels, body(): pl.pallas_call(kernel, out_shape=jax.ShapeDtypeStruct(hidden.shape, BF16)...  81.2 us

profile of v3, /device:TPU:0, one launch (start us, length us, event | category | flops | bytes accessed | tf_op | source)
XLA Modules:
  0.0 82.8 jit_solution(5125390406993158734)
XLA Ops:
  0.0 81.2 %layers.1 = bf16[1,16,4096]{2,1,0:T(8,128)(2,1)} custom-call(bf16[1,16,4096]{2,1,0:T(8,128)(2,1)} %hid.1, bf16[1,64,4096]{2,1,0:T(8,128)(2,1)} %vis.1, s32[1,16]{1,0:T(1,128)} %pos.1, s32[1,4,16]{2,1,0:T(4,128)} %bitcast.1, f32[1,128]{1,0:T(1,128)} %constant.2.clone.freq, bf16[4096]{0:T(1024)(128)(2,1)} %ln1a.1, bf16[4096,1024]{1,0:T(8,128)(2,1)} %wqa.1, ...), custom_call_target="tpu_custom_call" | custom-call | flops 13958643712 | bytes 218103808 | tf_op jit(solution)/shard_map/layers/pallas_call | solution.py:488
  81.3 1.6 %copy.28 = bf16[1,16,4096]{2,1,0:T(8,128)(2,1)} copy(bf16[1,16,4096]{2,1,0:T(8,128)(2,1)} %layers.1) | data formatting | bytes 262144

commit v4 on v3

--- a/solution.py
+++ b/solution.py
@@ -29,6 +29,7 @@
 FF = 3584
 NC = 256
 SP = 13
+EARLY = 6
 WO_ROWS = KV * REP * HD
 
 SEGMENTS = []
@@ -71,7 +72,7 @@
            ln1b, wqb, qn, wkb, wvb, kn, wob, ln2b, wgb, wub, wdb, xg,
            out,
            wbuf, wsem, hx, posb, maskb, cosb, sinb, visb, keepb, h, x, act, ctx, qb, kb, vb, vg,
-           pb, rcv1, snd2, rcv2, pf, rcvf, obuf, osem,
+           pb, rcv1, snd2, rcv2, pf, rcvf, obuf, osem, gbuf, ssq, rbuf, acc,
            lsem, hs, hr, ps, pr, ms, mr, vs, vr, s1, r1, s2, r2, s3, r3, fs, fr):
     d = lax.axis_index('tp')
     core = lax.rem(d, 2)
@@ -193,6 +194,9 @@
             visb[rows, tile * (V // 4):(tile + 1) * (V // 4)] = jnp.broadcast_to(as_column(seen[tile:tile + 1]), (TB, V // 4))
         keepb[rows, :] = jnp.broadcast_to(as_column(jnp.max(seen, axis=0, keepdims=True)), (TB, HD))
 
+    for k, gain in enumerate((ln1a, ln2a, ln1b, ln2b)):
+        for c in range(D // NC):
+            gbuf[k, c] = gain[pl.ds(c * NC, NC)].astype(F32).reshape(1, NC)
     own_vis.wait()
     for n in range(2):
         hid_half(cross, n, 1 + n, cross).wait_recv()
@@ -203,18 +207,20 @@
     for n in range(2):
         hid_half(diag, n, 3 + n, part).wait_recv()
 
+    def take(c, value, gain):
+        v = value.astype(F32)
+        x[:, cols(c)] = (v * gbuf[gain, c]).astype(BF16)
+        ssq[...] += v * v
+
+    def row_scale():
+        scale = lax.rsqrt(jnp.sum(ssq[...], axis=1, keepdims=True) * (1.0 / D) + NORM_EPS)
+        rbuf[...] = jnp.broadcast_to(scale, (T, HD))
+
+    ssq[...] = jnp.zeros((T, NC), F32)
     for c in range(D // NC):
         h[c] = hx[:, :, c * NC:(c + 1) * NC].reshape(T, NC)
-
-    def normalise(gain):
-        total = jnp.zeros((T, NC), F32)
-        for c in range(D // NC):
-            v = h[c].astype(F32)
-            total = total + v * v
-        scale = lax.rsqrt(jnp.sum(total, axis=1, keepdims=True) * (1.0 / D) + NORM_EPS)
-        for c in range(D // NC):
-            g = gain[pl.ds(c * NC, NC)].astype(F32).reshape(1, NC)
-            x[:, c * NC:(c + 1) * NC] = (h[c].astype(F32) * scale * g).astype(BF16)
+        take(c, h[c], 0)
+    row_scale()
 
     def head_norm(v, gain):
         scale = lax.rsqrt(jnp.mean(v * v, axis=1, keepdims=True) + NORM_EPS)
@@ -236,7 +242,7 @@
                 head = g * REP + r
                 ctx[:, head * HD:(head + 1) * HD] = o[r * T:(r + 1) * T]
 
-    def spread(parity, partials, update, between=None):
+    def spread(parity, partials, update, gain, first, count, between=None):
         def hop1(i):
             return remote(pb.at[1 - core, i], rcv1.at[i], s1.at[i], r1.at[i], part)
 
@@ -270,18 +276,46 @@
         if between is not None:
             between()
 
-        def final(i, carry):
+        def final(i):
             hop2(i).wait_recv()
             total = snd2[i].astype(F32) + rcv2[parity, i].astype(F32)
             mine = core * 8 + i
-            h[mine] = (h[mine].astype(F32) + update(total)).astype(BF16)
+            value = (h[mine].astype(F32) + update(total)).astype(BF16)
+            h[mine] = value
             hop3(core, i).start()
+            take(mine, value, gain)
+
+        ssq[...] = jnp.zeros((T, NC), F32)
+        for e in range(count):
+            for half in range(2):
+                acc[e, half] = jnp.zeros((T, NC), F32)
+            arrive(first + e)
+        final(0)
+        final(1)
+
+        def stage(n, carry):
+            @pl.when(n < 3)
+            def _():
+                final(2 * n + 2)
+                final(2 * n + 3)
+            for k in range(2):
+                i = 2 * n + k
+                theirs = (1 - core) * 8 + i
+                hop3(1 - core, i).wait_recv()
+                take(theirs, h[theirs], gain)
+            low = pl.ds(pl.multiple_of(n * 2 * NC, 2 * NC), 2 * NC)
+            high = pl.ds(pl.multiple_of(n * 2 * NC + D // 2, 2 * NC), 2 * NC)
+            x_low, x_high = x[:, low], x[:, high]
+            for e in range(count):
+                slot = (first + e) % SP
+                for half in range(2):
+                    acc[e, half] += dot(x_low, wbuf[slot, half, low]) + dot(x_high, wbuf[slot, half, high])
             return carry
 
-        lax.fori_loop(0, 8, final, 0)
+        lax.fori_loop(0, 4, stage, 0)
+        row_scale()
 
         def finish(i, carry):
-            hop3(1 - core, i).wait_recv()
             hop3(core, i).wait_send()
             hop1(i).wait_send()
             hop2(i).wait_send()
@@ -321,29 +355,32 @@
         return partials
 
     def mlp_up(base):
+        def activate(i, gate, up):
+            gate = gate * rbuf[:, 0:1]
+            act[:, cols(i)] = (gate * jax.nn.sigmoid(gate) * (up * rbuf[:, 0:1])).astype(BF16)
+
+        for e in range(EARLY):
+            activate(e, acc[e, 0], acc[e, 1])
+            refill(base + e, base + e, base + e + 1)
+
         def step(i, carry):
             slots = [arrive(base + 2 * i + n) for n in range(2)]
             for n, slot in enumerate(slots):
-                gate = dot(x[...], wbuf[slot, 0])
-                up = dot(x[...], wbuf[slot, 1])
-                act[:, cols(2 * i + n)] = (gate * jax.nn.sigmoid(gate) * up).astype(BF16)
+                activate(2 * i + n, dot(x[...], wbuf[slot, 0]), dot(x[...], wbuf[slot, 1]))
             for n in range(2):
-                refill(base + 2 * i + n, base, base + 14)
+                refill(base + 2 * i + n, base + EARLY, base + 14)
             return carry
-        lax.fori_loop(0, 7, step, 0)
-
-    def queries(base, finish):
-        slots = [arrive(base + i) for i in range(2)]
-        for i, slot in enumerate(slots):
-            for half in range(2):
-                q = dot(x[...], wbuf[slot, half])
-                for sub in range(2):
-                    qb[4 * i + 2 * half + sub] = finish(q[:, sub * HD:(sub + 1) * HD]).astype(BF16)
-
-    normalise(ln1a)
-    slot_kv = arrive(BASE['kva'])
-    queries(BASE['qa'], rope)
-    keys, vals = dot(x[...], wbuf[slot_kv, 0]), dot(x[...], wbuf[slot_kv, 1])
+        lax.fori_loop(EARLY // 2, 7, step, 0)
+
+    def queries(products, finish):
+        for n, q in enumerate(products):
+            q = q * rbuf[:, 0:1]
+            for sub in range(2):
+                qb[2 * n + sub] = finish(q[:, sub * HD:(sub + 1) * HD]).astype(BF16)
+
+    slots_a = [arrive(m) for m in range(3)]
+    queries([dot(x[...], wbuf[slot, half]) for slot in slots_a[:2] for half in range(2)], rope)
+    keys, vals = [dot(x[...], wbuf[slots_a[2], half]) * rbuf[:, 0:1] for half in range(2)]
     for g in range(KV):
         kb[g, pl.ds(0, T)] = rope(keys[:, g * HD:(g + 1) * HD]).astype(BF16)
         vb[g, pl.ds(0, T)] = vals[:, g * HD:(g + 1) * HD].astype(BF16)
@@ -351,13 +388,21 @@
         refill(m, m, m + 1)
     query_at = lax.rem(lax.broadcasted_iota(jnp.int32, (REP * T, T), 0), T)
     attend(T, query_at >= lax.broadcasted_iota(jnp.int32, (REP * T, T), 1))
-    spread(0, wo_partials(BASE['oa']), lambda total: total)
-    vis_half(d, 1, 2, cross).start()
-    normalise(ln2a)
+
+    def vision_send():
+        vis_half(d, 1, 2, cross).start()
+
+    spread(0, wo_partials(BASE['oa']), lambda total: total, 1, BASE['gua'], EARLY, vision_send)
     mlp_up(BASE['gua'])
-    for n in range(2):
-        vis_half(cross, n, 1 + n, cross).wait_recv()
-        vis_half(cross, n, 3 + n, part).start()
+    down_a = wd_partials(BASE['da'])
+
+    def down_and_forward(j):
+        @pl.when(j == 1)
+        def _():
+            for n in range(2):
+                vis_half(cross, n, 1 + n, cross).wait_recv()
+                vis_half(cross, n, 3 + n, part).start()
+        return down_a(j)
 
     def vision_heads():
         remote(vg.at[part], vg.at[part], vs.at[0], vr.at[0], part).wait_recv()
@@ -378,16 +423,14 @@
         lax.fori_loop(0, 2, kv_step, 0)
         refill(BASE['kvb'], BASE['kvb'], BASE['kvb'] + 1)
 
-    spread(1, wd_partials(BASE['da']), lambda total: total, vision_heads)
-
-    normalise(ln1b)
-    queries(BASE['qb'], lambda q: head_norm(q, qn))
+    spread(1, down_and_forward, lambda total: total, 2, BASE['qb'], 2, vision_heads)
+
+    queries([acc[e, half] for e in range(2) for half in range(2)], lambda q: head_norm(q, qn))
     for i in range(2):
         refill(BASE['qb'] + i, BASE['qb'] + i, BASE['qb'] + i + 1)
     attend(V, jnp.concatenate([visb[...]] * REP, axis=0) > 0.0)
     gate0 = jnp.tanh(jnp.full((T, 1), xg[0], F32)) * keepb[:, 0:1]
-    spread(2, wo_partials(BASE['ob']), lambda total: gate0 * total)
-    normalise(ln2b)
+    spread(2, wo_partials(BASE['ob']), lambda total: gate0 * total, 3, BASE['gub'], EARLY)
     mlp_up(BASE['gub'])
 
     own = pl.ds(pl.multiple_of(d * TB, TB), TB)
@@ -472,6 +515,8 @@
         pltpu.VMEM((8, 4, 2, TB, NC), BF16),
         pltpu.VMEM((8, 3, 2, TB, NC), BF16),
         pltpu.VMEM((TB, D), BF16), dma((8, 2)),
+        pltpu.VMEM((4, D // NC, 1, NC), F32), pltpu.VMEM((T, NC), F32), pltpu.VMEM((T, HD), F32),
+        pltpu.VMEM((EARLY, 2, T, NC), F32),
         dma((4,)),
         dma((5,)), dma((5,)), dma((3,)), dma((3,)), dma((3,)), dma((3,)),
         dma((5,)), dma((5,)),

time: 83 us -> 77.4 us (0.933)
  Pallas kernels: 81.2 us -> 75.6 us
    pallas_call x1, Pallas kernels: 81.2 us -> 75.6 us  [body(): pl.pallas_call(kernel, out_shape=jax.ShapeDtypeStruct(hidden.shape, BF16)...]
where the time goes in v4:
time: 77.4 us; the launch traced here: 77.2 us
  Pallas kernels  75.6 us (98%)
  local copies, waits for them, and re-layouts  1.57 us (2%)
    pallas_call x1, Pallas kernels, body(): pl.pallas_call(kernel, out_shape=jax.ShapeDtypeStruct(hidden.shape, BF16)...  75.6 us
    unnamed x1, local copies, waits for them, and re-layouts  1.57 us

profile of v4, /device:TPU:0, one launch (start us, length us, event | category | flops | bytes accessed | tf_op | source)
XLA Modules:
  0.0 77.2 jit_solution(5032593247010926134)
XLA Ops:
  0.0 75.6 %layers.1 = bf16[1,16,4096]{2,1,0:T(8,128)(2,1)} custom-call(bf16[1,16,4096]{2,1,0:T(8,128)(2,1)} %hid.1, bf16[1,64,4096]{2,1,0:T(8,128)(2,1)} %vis.1, s32[1,16]{1,0:T(1,128)} %pos.1, s32[1,4,16]{2,1,0:T(4,128)} %bitcast.1, f32[1,128]{1,0:T(1,128)} %constant.2.clone.freq, bf16[4096]{0:T(1024)(128)(2,1)} %ln1a.1, bf16[4096,1024]{1,0:T(8,128)(2,1)} %wqa.1, ...), custom_call_target="tpu_custom_call" | custom-call | flops 13958643712 | bytes 218103808 | tf_op jit(solution)/shard_map/layers/pallas_call | solution.py:533
  75.7 1.6 %copy.28 = bf16[1,16,4096]{2,1,0:T(8,128)(2,1)} copy(bf16[1,16,4096]{2,1,0:T(8,128)(2,1)} %layers.1) | data formatting | bytes 262144

commit v5 on v4

--- a/solution.py
+++ b/solution.py
@@ -67,12 +67,13 @@
     return lax.dot_general(a, b, (((1,), (1,)), ((), ())), preferred_element_type=F32)
 
 
-def kernel(hid, vis, pos, tmask, freq,
-           ln1a, wqa, wka, wva, woa, ln2a, wga, wua, wda,
-           ln1b, wqb, qn, wkb, wvb, kn, wob, ln2b, wgb, wub, wdb, xg,
+def kernel(hid, vis, pos, tmask, freq_hbm,
+           ln1a_hbm, wqa, wka, wva, woa, ln2a_hbm, wga, wua, wda,
+           ln1b_hbm, wqb, qn_hbm, wkb, wvb, kn_hbm, wob, ln2b_hbm, wgb, wub, wdb, xg_hbm,
            out,
            wbuf, wsem, hx, posb, maskb, cosb, sinb, visb, keepb, h, x, act, ctx, qb, kb, vb, vg,
            pb, rcv1, snd2, rcv2, pf, rcvf, obuf, osem, gbuf, ssq, rbuf, acc,
+           freq, ln1a, ln2a, ln1b, ln2b, qn, kn, xg, psem,
            lsem, hs, hr, ps, pr, ms, mr, vs, vr, s1, r1, s2, r2, s3, r3, fs, fr):
     d = lax.axis_index('tp')
     core = lax.rem(d, 2)
@@ -145,25 +146,38 @@
     own_mask.start()
     own_vis = pltpu.make_async_copy(vis.at[0], vg.at[d], lsem.at[3])
     own_vis.start()
+    small = [pltpu.make_async_copy(src, dst, psem.at[n]) for n, (src, dst) in enumerate((
+        (freq_hbm, freq), (ln1a_hbm, ln1a), (ln2a_hbm, ln2a), (ln1b_hbm, ln1b), (ln2b_hbm, ln2b),
+        (qn_hbm, qn), (kn_hbm, kn), (xg_hbm, xg)))]
     barrier = pltpu.get_barrier_semaphore()
     for peer in peers:
         pl.semaphore_signal(barrier, inc=1, device_id={'tp': peer}, device_id_type=MESH)
-    for m in range(4):
+    issue(0, 0, 1)
+    for copy in small:
+        copy.start()
+    for m in range(1, 4):
         issue(m, m, m + 1)
     own_rows.wait()
     own_pos.wait()
     own_mask.wait()
     pl.semaphore_wait(barrier, 3)
 
-    def hid_half(block, n, index, to):
-        rows = pl.ds(n * (TB // 2), TB // 2)
-        return remote(hx.at[block, rows], hx.at[block, rows], hs.at[index], hr.at[index], to)
+    def half_cols(n):
+        return pl.ds(pl.multiple_of(n * (D // 2), D // 2), D // 2)
+
+    def hid_cross(block, n):
+        piece = hx.at[block, :, half_cols(n)]
+        return remote(piece, piece, hs.at[1 + n], hr.at[1 + n], cross)
+
+    def hid_relay(block, n):
+        piece = hx.at[block, :, half_cols(n)]
+        return remote(piece, piece, hs.at[5 + n], hr.at[5 + n], part)
 
     def vis_half(block, n, index, to):
         rows = pl.ds(n * (VB // 2), VB // 2)
         return remote(vg.at[block, rows], vg.at[block, rows], vs.at[index], vr.at[index], to)
 
-    first_sends = [hid_half(d, 0, 1, cross), hid_half(d, 1, 2, cross), remote(hx.at[d], hx.at[d], hs.at[0], hr.at[0], part)]
+    first_sends = [hid_cross(d, n) for n in range(2)] + [remote(hx.at[d], hx.at[d], hs.at[0], hr.at[0], part)]
     for k, peer in enumerate(peers):
         first_sends.append(remote(posb.at[d], posb.at[d], ps.at[k], pr.at[k], peer))
         first_sends.append(remote(maskb.at[d], maskb.at[d], ms.at[k], mr.at[k], peer))
@@ -176,6 +190,9 @@
     for k, peer in enumerate(peers):
         remote(posb.at[peer], posb.at[peer], ps.at[k], pr.at[k], peer).wait_recv()
         remote(maskb.at[peer], maskb.at[peer], ms.at[k], mr.at[k], peer).wait_recv()
+
+    for copy in small:
+        copy.wait()
 
     sign = jnp.where(lax.broadcasted_iota(jnp.int32, (TB, HD), 1) < HD // 2, -1.0, 1.0)
     eye = lax.broadcasted_iota(jnp.int32, (TB, TB), 0) == lax.broadcasted_iota(jnp.int32, (TB, TB), 1)
@@ -197,15 +214,6 @@
     for k, gain in enumerate((ln1a, ln2a, ln1b, ln2b)):
         for c in range(D // NC):
             gbuf[k, c] = gain[pl.ds(c * NC, NC)].astype(F32).reshape(1, NC)
-    own_vis.wait()
-    for n in range(2):
-        hid_half(cross, n, 1 + n, cross).wait_recv()
-        hid_half(cross, n, 3 + n, part).start()
-    vis_part.start()
-    vis_half(d, 0, 1, cross).start()
-    remote(hx.at[part], hx.at[part], hs.at[0], hr.at[0], part).wait_recv()
-    for n in range(2):
-        hid_half(diag, n, 3 + n, part).wait_recv()
 
     def take(c, value, gain):
         v = value.astype(F32)
@@ -217,9 +225,31 @@
         rbuf[...] = jnp.broadcast_to(scale, (T, HD))
 
     ssq[...] = jnp.zeros((T, NC), F32)
-    for c in range(D // NC):
-        h[c] = hx[:, :, c * NC:(c + 1) * NC].reshape(T, NC)
-        take(c, h[c], 0)
+    for e in range(3):
+        for half in range(2):
+            acc[e, half] = jnp.zeros((T, NC), F32)
+        arrive(e)
+    for n in range(2):
+        hid_cross(cross, n).wait_recv()
+        hid_relay(cross, n).start()
+    own_vis.wait()
+    vis_part.start()
+    vis_half(d, 0, 1, cross).start()
+    remote(hx.at[part], hx.at[part], hs.at[0], hr.at[0], part).wait_recv()
+
+    def first_stage(n, carry):
+        hid_relay(diag, n).wait_recv()
+        for k in range(8):
+            c = 8 * n + k
+            h[c] = hx[:, :, cols(c)].reshape(T, NC)
+            take(c, h[c], 0)
+        x_part = x[:, half_cols(n)]
+        for e in range(3):
+            for half in range(2):
+                acc[e, half] += dot(x_part, wbuf[e, half, half_cols(n)])
+        return carry
+
+    lax.fori_loop(0, 2, first_stage, 0)
     row_scale()
 
     def head_norm(v, gain):
@@ -289,7 +319,6 @@
         for e in range(count):
             for half in range(2):
                 acc[e, half] = jnp.zeros((T, NC), F32)
-            arrive(first + e)
         final(0)
         final(1)
 
@@ -298,6 +327,11 @@
             def _():
                 final(2 * n + 2)
                 final(2 * n + 3)
+
+            @pl.when(n == 0)
+            def _():
+                for e in range(count):
+                    arrive(first + e)
             for k in range(2):
                 i = 2 * n + k
                 theirs = (1 - core) * 8 + i
@@ -342,15 +376,15 @@
             return out
         return partials
 
-    def wd_partials(base):
+    def wd_partials(base, count=2):
         def partials(j):
-            slots = [arrive(base + 2 * j + n, FF) for n in range(2)]
+            slots = [arrive(base + count * j + n, FF) for n in range(count)]
             out = []
             for slot in slots:
                 rows = pl.ds(0, FF)
                 out.append((dot(act[...], wbuf[slot, 0, rows]), dot(act[...], wbuf[slot, 1, rows])))
-            for n in range(2):
-                refill(base + 2 * j + n, base, base + 8)
+            for n in range(count):
+                refill(base + count * j + n, base, base + 8)
             return out
         return partials
 
@@ -378,9 +412,8 @@
             for sub in range(2):
                 qb[2 * n + sub] = finish(q[:, sub * HD:(sub + 1) * HD]).astype(BF16)
 
-    slots_a = [arrive(m) for m in range(3)]
-    queries([dot(x[...], wbuf[slot, half]) for slot in slots_a[:2] for half in range(2)], rope)
-    keys, vals = [dot(x[...], wbuf[slots_a[2], half]) * rbuf[:, 0:1] for half in range(2)]
+    queries([acc[e, half] for e in range(2) for half in range(2)], rope)
+    keys, vals = [acc[2, half] * rbuf[:, 0:1] for half in range(2)]
     for g in range(KV):
         kb[g, pl.ds(0, T)] = rope(keys[:, g * HD:(g + 1) * HD]).astype(BF16)
         vb[g, pl.ds(0, T)] = vals[:, g * HD:(g + 1) * HD].astype(BF16)
@@ -435,18 +468,16 @@
 
     own = pl.ds(pl.multiple_of(d * TB, TB), TB)
     gate1 = jnp.tanh(jnp.full((TB, 1), xg[1], F32)) * keepb[own, 0:1]
-    down = wd_partials(BASE['db'])
+    down = wd_partials(BASE['db'], 1)
 
     def last_step(j, carry):
-        for n, values in enumerate(down(j)):
-            i = 2 * j + n
-            for half, value in enumerate(values):
-                pf[i, :, half] = value.astype(BF16).reshape(4, TB, NC)
-            for k, peer in enumerate(peers):
-                remote(pf.at[i, peer], rcvf.at[i, k], fs.at[i, k], fr.at[i, k], peer).start()
+        for half, value in enumerate(down(j)[0]):
+            pf[j, :, half] = value.astype(BF16).reshape(4, TB, NC)
+        for k, peer in enumerate(peers):
+            remote(pf.at[j, peer], rcvf.at[j, k], fs.at[j, k], fr.at[j, k], peer).start()
         return carry
 
-    lax.fori_loop(0, 4, last_step, 0)
+    lax.fori_loop(0, 8, last_step, 0)
 
     def last_sum(i, carry):
         for k, peer in enumerate(peers):
@@ -466,7 +497,7 @@
         copy.wait_send()
     vis_part.wait_send()
     for n in range(2):
-        hid_half(cross, n, 3 + n, part).wait_send()
+        hid_relay(cross, n).wait_send()
         vis_half(d, n, 1 + n, cross).wait_send()
         vis_half(cross, n, 3 + n, part).wait_send()
 
@@ -491,8 +522,6 @@
     table = rope_table(HD)
 
     hbm = pl.BlockSpec(memory_space=pl.ANY)
-    vmem = pl.BlockSpec(memory_space=pltpu.VMEM)
-    smem = pl.BlockSpec(memory_space=pltpu.SMEM)
     dma = pltpu.SemaphoreType.DMA
     scratch = [
         pltpu.VMEM((SP, 2, D, NC), BF16), dma((SP, 2)),
@@ -517,8 +546,10 @@
         pltpu.VMEM((TB, D), BF16), dma((8, 2)),
         pltpu.VMEM((4, D // NC, 1, NC), F32), pltpu.VMEM((T, NC), F32), pltpu.VMEM((T, HD), F32),
         pltpu.VMEM((EARLY, 2, T, NC), F32),
+        pltpu.VMEM((1, HD), F32), pltpu.VMEM((D,), BF16), pltpu.VMEM((D,), BF16), pltpu.VMEM((D,), BF16), pltpu.VMEM((D,), BF16),
+        pltpu.VMEM((HD,), BF16), pltpu.VMEM((HD,), BF16), pltpu.SMEM((2,), F32), dma((8,)),
         dma((4,)),
-        dma((5,)), dma((5,)), dma((3,)), dma((3,)), dma((3,)), dma((3,)),
+        dma((9,)), dma((9,)), dma((3,)), dma((3,)), dma((3,)), dma((3,)),
         dma((5,)), dma((5,)),
         dma((8,)), dma((8,)), dma((3, 8)), dma((3, 8)), dma((8,)), dma((8,)),
         dma((8, 3)), dma((8, 3)),
@@ -526,10 +557,7 @@
 
     def body(hidden, vision, positions, tile_mask, *params):
         freqs = jnp.asarray(np.concatenate([table, table])[None])
-        specs = [hbm, hbm, hbm, hbm, vmem]
-        for k, p in enumerate(params):
-            specs.append(vmem if p.ndim == 1 else hbm)
-        specs[-1] = smem
+        specs = [hbm] * (5 + len(params))
         return pl.pallas_call(
             kernel,
             out_shape=jax.ShapeDtypeStruct(hidden.shape, BF16),

time: 77.4 us -> 77 us (level)
  no operation moved by 1% of the time
where the time goes in v5:
time: 77 us; the launch traced here: 76.9 us
  Pallas kernels  75.3 us (98%)
  local copies, waits for them, and re-layouts  1.57 us (2%)
    pallas_call x1, Pallas kernels, body(): pl.pallas_call(kernel, out_shape=jax.ShapeDtypeStruct(hidden.shape, BF16)...  75.3 us
    unnamed x1, local copies, waits for them, and re-layouts  1.57 us

profile of v5, /device:TPU:0, one launch (start us, length us, event | category | flops | bytes accessed | tf_op | source)
XLA Modules:
  0.0 76.9 jit_solution(1049539942060999349)
XLA Ops:
  0.0 75.3 %layers.1 = bf16[1,16,4096]{2,1,0:T(8,128)(2,1)} custom-call(bf16[1,16,4096]{2,1,0:T(8,128)(2,1)} %hid.1, bf16[1,64,4096]{2,1,0:T(8,128)(2,1)} %vis.1, s32[1,16]{1,0:T(1,128)} %pos.1, s32[1,4,16]{2,1,0:T(4,128)} %bitcast.1, f32[1,128]{1,0:T(1,128)} %constant.2.clone.freq_hbm, bf16[4096]{0:T(1024)(128)(2,1)} %ln1a_hbm.1, bf16[4096,1024]{1,0:T(8,128)(2,1)} %wqa.1, ...), custom_call_target="tpu_custom_call" | custom-call | flops 13958643712 | bytes 218103808 | tf_op jit(solution)/shard_map/layers/pallas_call | solution.py:561
  75.3 1.6 %copy.28 = bf16[1,16,4096]{2,1,0:T(8,128)(2,1)} copy(bf16[1,16,4096]{2,1,0:T(8,128)(2,1)} %layers.1) | data formatting | bytes 262144
